TPU v7x, 16 devices: a whole 2x2x2 slice. The times are simulated.
16 devices in a mesh: dp: 2 (over z), tp: 8 (over y, x, core).
Axes of the slice: x: 2, y: 2, z: 2, core: 2. Of those that a mesh axis runs over, the one named last changes fastest.
Arguments:
- layer_in: bfloat16 [32, 256, 4096], P('dp', 'tp'), parts along dimension 0
- grad_out: bfloat16 [32, 256, 4096], P('dp', 'tp'), parts along dimension 0
- w_qkv: bfloat16 [4096, 32, 3, 128], P(None, 'tp')
- w_out: bfloat16 [32, 1, 128, 4096], P('tp')
- w_up: bfloat16 [4096, 16384], P(None, 'tp')
- w_down: bfloat16 [16384, 4096], P('tp')
- ln_params: float32 [4, 4096], replicated
Outputs:
- output 1: bfloat16 [32, 256, 4096], P('dp', 'tp'), parts along dimension 0
- output 2: bfloat16 [8192, 32, 3, 128], P('dp', 'tp'), parts along dimension 0
- output 3: bfloat16 [64, 1, 128, 4096], P(('dp', 'tp')), parts along dimension 0
- output 4: bfloat16 [8192, 16384], P('dp', 'tp'), parts along dimension 0
- output 5: bfloat16 [32768, 4096], P(('dp', 'tp')), parts along dimension 0
- output 6: float32 [8, 4096], P('dp'), parts along dimension 0
There are 2 independent parts. A program takes and returns all parts, laid end to end along the dimension named above; an argument that names none is the same for every part.
All inputs are finite; a program needn't handle non-finite values.
Results may differ from a plain program's by a relative error of at most 0.0074571.
Values are sent between devices in bfloat16 or wider.
A program may use at most 1 GiB of HBM per device.

v0:
```python
import jax
import jax.numpy as jnp
from jax import lax
from jax.sharding import PartitionSpec as P

NORM_EPS = 1e-5
ROPE_BASE = 10000.0
NEG_BIG = -1e30


def norm_stats(source):
    widened = source.astype(jnp.float32)
    centred = widened - jnp.mean(widened, axis=-1, keepdims=True)
    inv_std = lax.rsqrt(jnp.mean(centred * centred, axis=-1, keepdims=True) + NORM_EPS)
    return centred * inv_std, inv_std


def norm_backward(cotangent, normed, inv_std, gain_row):
    scaled = cotangent * gain_row
    return inv_std * (scaled - jnp.mean(scaled, axis=-1, keepdims=True) - normed * jnp.mean(scaled * normed, axis=-1, keepdims=True))


def rope_tables(seq_len, head_dim):
    half_dim = head_dim // 2
    inv_freq = ROPE_BASE ** (-2.0 * jnp.arange(half_dim, dtype=jnp.float32) / head_dim)
    angles = jnp.arange(seq_len, dtype=jnp.float32)[:, None] * inv_freq[None, :]
    angles = jnp.concatenate([angles, angles], axis=-1)
    return jnp.cos(angles), jnp.sin(angles)


def rotate_half(tensor):
    half_dim = tensor.shape[-1] // 2
    return jnp.concatenate([-tensor[..., half_dim:], tensor[..., :half_dim]], axis=-1)


def rotate_half_back(tensor):
    half_dim = tensor.shape[-1] // 2
    return jnp.concatenate([tensor[..., half_dim:], -tensor[..., :half_dim]], axis=-1)


def apply_rope(tensor, cos_tab, sin_tab):
    widened = tensor.astype(jnp.float32)
    return (widened * cos_tab + rotate_half(widened) * sin_tab).astype(jnp.bfloat16)


def rope_backward(cotangent, cos_tab, sin_tab):
    return cotangent * cos_tab + rotate_half_back(cotangent * sin_tab)


def exact_gelu(pre_vals):
    return jax.nn.gelu(pre_vals, approximate=False)


def attention_backward(queries, key_rot, val_rows, ctx_grad):
    seq_len = queries.shape[1]
    score_scale = queries.shape[-1] ** -0.5
    positions = jnp.arange(seq_len)
    causal = positions[:, None] >= positions[None, :]
    scores = jnp.einsum('bqgjh,bkgh->bgjqk', queries, key_rot, preferred_element_type=jnp.float32) * score_scale
    scores = jnp.where(causal, scores, NEG_BIG)
    attn_probs = jax.nn.softmax(scores, axis=-1)
    probs_bf16 = attn_probs.astype(jnp.bfloat16)
    context = jnp.einsum('bgjqk,bkgh->bqgjh', probs_bf16, val_rows, preferred_element_type=jnp.float32).astype(jnp.bfloat16)
    prob_grad = jnp.einsum('bqgjh,bkgh->bgjqk', ctx_grad, val_rows, preferred_element_type=jnp.float32)
    val_grad = jnp.einsum('bgjqk,bqgjh->bkgh', probs_bf16, ctx_grad, preferred_element_type=jnp.float32)
    score_grad = attn_probs * (prob_grad - jnp.sum(prob_grad * attn_probs, axis=-1, keepdims=True))
    score_grad = (score_grad * score_scale).astype(jnp.bfloat16)
    query_grad = jnp.einsum('bgjqk,bkgh->bqgjh', score_grad, key_rot, preferred_element_type=jnp.float32)
    key_grad = jnp.einsum('bgjqk,bqgjh->bkgh', score_grad, queries, preferred_element_type=jnp.float32)
    return context, query_grad, key_grad, val_grad


def branch_grads(attn_in, mlp_in, full_grad, w_qkv, w_out, w_up, w_down):
    group_size = w_out.shape[1]
    seq_len = attn_in.shape[1]
    proj_qkv = jnp.einsum('bsd,dgth->bsgth', attn_in, w_qkv, preferred_element_type=jnp.float32).astype(jnp.bfloat16)
    cos_tab, sin_tab = rope_tables(seq_len, w_qkv.shape[-1])
    cos_q = cos_tab[:, None, None, :]
    sin_q = sin_tab[:, None, None, :]
    cos_k = cos_tab[:, None, :]
    sin_k = sin_tab[:, None, :]
    queries = apply_rope(proj_qkv[:, :, :, :group_size], cos_q, sin_q)
    key_rot = apply_rope(proj_qkv[:, :, :, group_size], cos_k, sin_k)
    val_rows = proj_qkv[:, :, :, group_size + 1]
    ctx_grad = jnp.einsum('bsd,gjhd->bsgjh', full_grad, w_out, preferred_element_type=jnp.float32).astype(jnp.bfloat16)
    context, query_grad, key_grad, val_grad = attention_backward(queries, key_rot, val_rows, ctx_grad)
    qkv_grad = jnp.concatenate([rope_backward(query_grad, cos_q, sin_q), rope_backward(key_grad, cos_k, sin_k)[:, :, :, None], val_grad[:, :, :, None]], axis=3).astype(jnp.bfloat16)
    attn_part = jnp.einsum('bsgth,dgth->bsd', qkv_grad, w_qkv, preferred_element_type=jnp.float32)
    grad_qkv = jnp.einsum('bsd,bsgth->dgth', attn_in, qkv_grad, preferred_element_type=jnp.float32).astype(jnp.bfloat16)
    grad_wout = jnp.einsum('bsgjh,bsd->gjhd', context, full_grad, preferred_element_type=jnp.float32).astype(jnp.bfloat16)
    pre_act = jnp.einsum('bsd,df->bsf', mlp_in, w_up, preferred_element_type=jnp.float32)
    act_vals, gelu_vjp = jax.vjp(exact_gelu, pre_act)
    act_grad = jnp.einsum('bsd,fd->bsf', full_grad, w_down, preferred_element_type=jnp.float32)
    hidden_grad = gelu_vjp(act_grad)[0].astype(jnp.bfloat16)
    grad_down = jnp.einsum('bsf,bsd->fd', act_vals.astype(jnp.bfloat16), full_grad, preferred_element_type=jnp.float32).astype(jnp.bfloat16)
    grad_up = jnp.einsum('bsd,bsf->df', mlp_in, hidden_grad, preferred_element_type=jnp.float32).astype(jnp.bfloat16)
    mlp_part = jnp.einsum('bsf,df->bsd', hidden_grad, w_up, preferred_element_type=jnp.float32)
    return attn_part, mlp_part, (grad_qkv, grad_wout, grad_up, grad_down)


def solution(mesh):
    act_spec = P('dp', 'tp', None)

    def device_step(layer_in, grad_out, w_qkv, w_out, w_up, w_down, ln_params):
        seq_local = layer_in.shape[1]
        full_in = lax.all_gather(layer_in, 'tp', axis=1, tiled=True)
        full_grad = lax.all_gather(grad_out, 'tp', axis=1, tiled=True)
        normed, inv_std = norm_stats(full_in)
        attn_in = (normed * ln_params[0] + ln_params[1]).astype(jnp.bfloat16)
        mlp_in = (normed * ln_params[2] + ln_params[3]).astype(jnp.bfloat16)
        attn_part, mlp_part, weight_grads = branch_grads(attn_in, mlp_in, full_grad, w_qkv, w_out, w_up, w_down)
        attn_cot = lax.psum_scatter(attn_part, 'tp', scatter_dimension=1, tiled=True)
        mlp_cot = lax.psum_scatter(mlp_part, 'tp', scatter_dimension=1, tiled=True)
        row_start = lax.axis_index('tp') * seq_local
        normed_loc = lax.dynamic_slice_in_dim(normed, row_start, seq_local, axis=1)
        inv_std_loc = lax.dynamic_slice_in_dim(inv_std, row_start, seq_local, axis=1)
        grad_in = (grad_out.astype(jnp.float32) + norm_backward(attn_cot, normed_loc, inv_std_loc, ln_params[0]) + norm_backward(mlp_cot, normed_loc, inv_std_loc, ln_params[2])).astype(jnp.bfloat16)
        ln_local = jnp.stack([jnp.sum(attn_cot * normed_loc, axis=(0, 1)), jnp.sum(attn_cot, axis=(0, 1)), jnp.sum(mlp_cot * normed_loc, axis=(0, 1)), jnp.sum(mlp_cot, axis=(0, 1))])
        grad_ln = lax.psum(ln_local, 'tp')
        return (grad_in,) + weight_grads + (grad_ln,)

    mapped = jax.shard_map(
        device_step,
        mesh=mesh,
        in_specs=(act_spec, act_spec, P(None, 'tp', None, None), P('tp', None, None, None), P(None, 'tp'), P('tp', None), P(None, None)),
        out_specs=(act_spec, P('dp', 'tp', None, None), P(('dp', 'tp'), None, None, None), P('dp', 'tp'), P(('dp', 'tp'), None), P('dp', None)),
        check_vma=False,
    )
    return mapped
```

profile of v0, /device:TPU:0, one launch (start us, length us, event | category | flops | bytes accessed | tf_op | source)
XLA Modules:
  0.0 1355.4 jit_solution(4766095930906743776)
XLA Ops:
  10.4 159.2 %all-gather.3.cloned.1.call-done = bf16[16,256,4096]{2,1,0:T(8,128)(2,1)} async-done(((bf16[16,32,4096]{2,1,0:T(8,128)(2,1)}), bf16[16,256,4096]{2,1,0:T(8,128)(2,1)}) %all-gather.3.cloned.1.call-update) | async-done | bytes 33554448 | tf_op jit(solution)/shard_map/all_gather | solution.py:106
  169.6 14.0 %convert_reduce_fusion = f32[16,256]{1,0:T(8,128)S(1)} fusion(bf16[16,256,4096]{2,1,0:T(8,128)(2,1)} %all-gather.3.cloned.1.call-done), kind=kLoop, calls=%fused_computation.1 | loop fusion | flops 33550336 | bytes 33570816 | tf_op jit(solution)/shard_map/reduce_sum | solution.py:13
  183.6 13.5 fusion.2
  197.2 88.6 %fusion.26 = (u16[256,2048]{1,0:T(8,128)(2,1)S(1)}, u16[256,2048]{1,0:T(8,128)(2,1)S(1)}, f32[16,256,2048]{2,1,0:T(8,128)}) fusion(bf16[4096,2048]{1,0:T(8,128)(2,1)} %param.11, f32[4096]{0:T(1024)S(1)} %bitcast.241, f32[4096]{0:T(1024)S(1)} %bitcast.233, f32[16,256]{1,0:T(8,128)S(1)} %add_rsqrt_fusion, f32[16,256]{1,0:T(8,128)S(1)} %broadcast_multiply_fusion, ...), kind=kOutput, calls=%fused_computation.53 | convolution fusion | flops 68928143360 | bytes 86048768 | tf_op jit(solution)/shard_map/bsd,df->bsf/dot_general | solution.py:91
  285.9 74.2 %fusion.3 = f32[16,256,2048]{2,1,0:T(8,128)} fusion(f32[16,256,2048]{2,1,0:T(8,128)} %get-tuple-element.40, u16[256,2048]{1,0:T(8,128)(2,1)S(1)} %get-tuple-element.19, u16[256,2048]{1,0:T(8,128)(2,1)S(1)} %get-tuple-element.18), kind=kLoop, calls=%fused_computation.9 | loop fusion | flops 562036736 | bytes 69206016 | tf_op jit(solution)/shard_map/jvp()/erfc | solution.py:51
  360.0 89.7 %add_convert_fusion.2 = bf16[16,256,2048]{2,1,0:T(8,128)(2,1)} fusion(f32[16,256,2048]{2,1,0:T(8,128)} %fusion.3, bf16[16,256,4096]{2,1,0:T(8,128)(2,1)} %all-gather.5.cloned.1.call-done, f32[16,256,2048]{2,1,0:T(8,128)} %get-tuple-element.40, bf16[2048,4096]{1,0:T(8,128)(2,1)} %param.12), kind=kOutput, calls=%fused_computation.23 | convolution fusion | flops 68836917248 | bytes 134217728 | tf_op jit(solution)/shard_map/bsd,fd->bsf/dot_general | solution.py:93
  449.8 79.1 %fusion.18 = f32[16,256,4096]{2,1,0:T(8,128)} fusion(bf16[16,256,2048]{2,1,0:T(8,128)(2,1)} %add_convert_fusion.2, bf16[4096,2048]{1,0:T(8,128)(2,1)} %param.11), kind=kOutput, calls=%fused_computation.42 | convolution fusion | flops 68719476736 | bytes 100663296 | tf_op jit(solution)/shard_map/bsf,df->bsd/dot_general | solution.py:97
  529.0 21.1 %copy.13 = bf16[4096,4,3,128]{0,3,2,1:T(8,128)(2,1)} copy(bf16[4096,4,3,128]{3,1,2,0:T(4,128)(2,1)} %param.9) | data formatting | bytes 25165824 | tf_op args[2]
  552.0 67.0 %fusion.47 = bf16[16,256,4,3,128]{1,4,3,2,0:T(8,128)(2,1)} fusion(bf16[4096,4,3,128]{0,3,2,1:T(8,128)(2,1)} %copy.13, f32[4096]{0:T(1024)S(1)} %bitcast.243, f32[4096]{0:T(1024)S(1)} %bitcast.229, f32[16,256]{1,0:T(8,128)S(1)} %copy-done.24, f32[16,256]{1,0:T(8,128)S(1)} %copy-done.16, bf16[16,256,4096]{2,1,0:T(8,128)(2,1)} %all-gather.3.cloned.1.call-done), kind=kOutput, calls=%fused_computation.89 | convolution fusion | flops 51646562304 | bytes 58785792 | tf_op jit(solution)/shard_map/bsd,dgth->bsgth/dot_general | solution.py:76
  619.0 12.3 slice_convert_fusion
  631.2 6.9 slice_negate_fusion.2
  655.5 8.1 fusion.29
  663.7 10.5 fusion.28
  674.2 22.8 %fusion.69 = bf16[16,256,4,128]{3,1,2,0:T(8,128)(2,1)} fusion(bf16[4,1,128,4096]{3,2,1,0:T(8,128)(2,1)S(1)} %copy-done.31, bf16[16,256,4096]{2,1,0:T(8,128)(2,1)} %all-gather.5.cloned.1.call-done), kind=kOutput, calls=%fused_computation.107 | convolution fusion | flops 17181966336 | bytes 41943040 | tf_op jit(solution)/shard_map/bsd,gjhd->bsgjh/dot_general | solution.py:85
  697.0 15.6 %fusion.21 = (f32[16,4,256]{2,1,0:T(4,128)S(1)}, f32[16,4,256,256]{3,2,1,0:T(8,128)}) fusion(f32[16,4,256]{2,1,0:T(4,128)S(1)} %fusion.28, f32[16,4,256]{2,1,0:T(4,128)S(1)} %get-tuple-element.41, f32[16,4,256,256]{3,2,1,0:T(8,128)} %get-tuple-element.42, pred[256,256]{0,1:T(8,128)(4,1)S(1)} %copy-done.9, bf16[16,256,4,128]{3,1,2,0:T(8,128)(2,1)} %fusion.69, ...), kind=kOutput, calls=%fused_computation.47 | convolution fusion | flops 1098891264 | bytes 42205184 | tf_op jit(solution)/shard_map/bqgjh,bkgh->bgjqk/dot_general | solution.py:64
  712.5 13.5 fusion.36
  726.1 10.0 bitcast_multiply_fusion.3
  740.4 14.1 %bitcast_multiply_fusion.1 = (f32[16,256,4,128]{1,3,2,0:T(8,128)}, f32[16,4,128,256]{3,2,1,0:T(8,128)}) fusion(f32[256,128]{0,1:T(8,128)S(1)} %copy-done.7, bf16[16,256,4,128]{1,3,2,0:T(8,128)(2,1)} %copy-done.2, bf16[16,4,256,256]{2,3,1,0:T(8,128)(2,1)} %copy-done), kind=kOutput, calls=%fused_computation.78 | convolution fusion | flops 1075838976 | bytes 29491200 | tf_op jit(solution)/shard_map/bgjqk,bqgjh->bkgh/dot_general | solution.py:69
  754.6 9.6 fusion.85
  775.8 10.4 convert_bitcast_fusion
  786.2 62.7 %convolution_bitcast_fusion = f32[16,256,4096]{2,1,0:T(8,128)} fusion(bf16[4096,4,3,128,1]{3,1,2,0,4:T(4,128)(2,1)} %bitcast.228, bf16[16,256,4,1,128]{1,4,3,2,0:T(8,128)(2,1)} %convert_bitcast_fusion, bf16[16,256,4,1,128]{1,4,3,2,0:T(8,128)(2,1)} %fusion.58, bf16[16,256,4,1,128]{1,4,3,2,0:T(8,128)(2,1)} %fusion.41), kind=kOutput, calls=%fused_computation.8 | convolution fusion | flops 51552190464 | bytes 92274688 | tf_op jit(solution)/shard_map/bsgth,dgth->bsd/dot_general | solution.py:88
  849.7 72.4 %bitcast_convert_fusion.2 = bf16[4096,4,3,128]{3,0,2,1:T(8,128)(2,1)} fusion(f32[4096]{0:T(1024)S(1)} %bitcast.244, f32[4096]{0:T(1024)S(1)} %bitcast.230, f32[16,256]{1,0:T(8,128)S(1)} %copy-done.25, f32[16,256]{1,0:T(8,128)S(1)} %copy-done.17, bf16[16,256,4096]{2,1,0:T(8,128)(2,1)} %all-gather.3.cloned.1.call-done, ...), kind=kOutput, calls=%fused_computation.36 | convolution fusion | flops 51684311040 | bytes 58785792 | tf_op jit(solution)/shard_map/bsd,bsgth->dgth/dot_general | solution.py:89
  922.1 17.4 %copy.30 = bf16[4096,4,3,128]{3,1,2,0:T(4,128)(2,1)} copy(bf16[4096,4,3,128]{3,0,2,1:T(8,128)(2,1)} %bitcast_convert_fusion.2) | data formatting | bytes 25165824
  940.2 14.2 %fusion.114 = bf16[16,256,4,128]{1,3,2,0:T(8,128)(2,1)S(1)} fusion(bf16[16,256,4,3,128]{1,4,3,2,0:T(8,128)(2,1)} %fusion.47, f32[16,4,256]{2,1,0:T(4,128)S(1)} %copy-done.14, f32[16,4,256]{2,1,0:T(4,128)S(1)} %copy-done.12, f32[16,4,256,256]{3,2,1,0:T(8,128)} %get-tuple-element.42, pred[256,256]{0,1:T(8,128)(4,1)S(1)} %copy-done.10), kind=kOutput, calls=%fused_computation.102.clone.1 | convolution fusion | flops 1096810496 | bytes 25362432 | tf_op jit(solution)/shard_map/bgjqk,bkgh->bqgjh/dot_general | solution.py:63
  954.4 27.4 %fusion.55 = bf16[4,1,128,4096]{3,2,1,0:T(8,128)(2,1)} fusion(bf16[16,256,4096]{2,1,0:T(8,128)(2,1)} %all-gather.5.cloned.1.call-done, bf16[16,256,4,128]{1,3,2,0:T(8,128)(2,1)S(1)} %fusion.114), kind=kOutput, calls=%fused_computation.91 | convolution fusion | flops 17181966336 | bytes 41943040 | tf_op jit(solution)/shard_map/bsgjh,bsd->gjhd/dot_general | solution.py:90
  981.8 37.1 %fusion = f32[16,256,4096]{2,1,0:T(8,128)} fusion(bf16[16,256,4096]{2,1,0:T(8,128)(2,1)} %all-gather.3.cloned.1.call-done, f32[16,256]{1,0:T(8,128)S(1)} %copy-done.25, f32[16,256]{1,0:T(8,128)S(1)} %copy-done.17), kind=kLoop, calls=%fused_computation.2 | loop fusion | flops 50331648 | bytes 100696064 | tf_op jit(solution)/shard_map/mul | solution.py:15
  1018.9 90.9 %bitcast_convert_fusion.1 = bf16[4096,2048]{1,0:T(8,128)(2,1)} fusion(bf16[16,256,2048]{2,1,0:T(8,128)(2,1)} %add_convert_fusion.2, f32[4096]{0:T(1024)S(1)} %bitcast.242, f32[4096]{0:T(1024)S(1)} %bitcast.234, f32[16,256]{1,0:T(8,128)S(1)} %copy-done.25, f32[16,256]{1,0:T(8,128)S(1)} %copy-done.17, bf16[16,256,4096]{2,1,0:T(8,128)(2,1)} %all-gather.3.cloned.1.call-done), kind=kOutput, calls=%fused_computation.17 | convolution fusion | flops 68828528640 | bytes 67174400 | tf_op jit(solution)/shard_map/bsd,bsf->df/dot_general | solution.py:96
  1109.8 86.8 %bitcast_convert_fusion = bf16[2048,4096]{1,0:T(8,128)(2,1)} fusion(bf16[16,256,4096]{2,1,0:T(8,128)(2,1)} %all-gather.5.cloned.1.call-done, f32[16,256,2048]{2,1,0:T(8,128)} %fusion.3, f32[16,256,2048]{2,1,0:T(8,128)} %get-tuple-element.40), kind=kOutput, calls=%fused_computation.16 | convolution fusion | flops 68753031168 | bytes 117440512 | tf_op jit(solution)/shard_map/bsf,bsd->fd/dot_general | solution.py:95
  1196.6 92.6 %reduce-scatter.3.cloned.1.call-done = f32[16,32,4096]{2,1,0:T(8,128)} async-done(((f32[16,256,4096]{2,1,0:T(8,128)}), f32[16,32,4096]{2,1,0:T(8,128)}) %reduce-scatter.3.cloned.1.call-update) | async-done | bytes 8388624 | tf_op jit(solution)/shard_map/reduce_scatter | solution.py:112
  1289.2 11.3 multiply_reduce_fusion.1
  1301.3 14.1 %add_convert_fusion.7 = bf16[16,32,4096]{2,1,0:T(8,128)(2,1)} fusion(bf16[16,32,4096]{2,1,0:T(8,128)(2,1)} %param.8, f32[16,32,4096]{2,1,0:T(8,128)} %reduce-scatter.5.cloned.1.call-done, f32[16,32,4096]{2,1,0:T(8,128)} %reduce-scatter.3.cloned.1.call-done, f32[16,256,4096]{2,1,0:T(8,128)} %fusion, s32[]{:T(128)S(6)} %select_n.8, ...), kind=kLoop, calls=%fused_computation.84 | loop fusion | flops 29360128 | bytes 33597444 | tf_op jit(solution)/shard_map/convert_element_type | solution.py:117
  1315.5 31.7 %all-reduce.2.cloned.1.call-done = f32[4,4096]{1,0:T(4,128)} async-done(((f32[4,4096]{1,0:T(4,128)}), f32[4,4096]{1,0:T(4,128)}) %all-reduce.2.cloned.1.call-update) | async-done | bytes 65552 | tf_op jit(solution)/shard_map/psum | solution.py:119
  (111 shorter events, 42.2 us)
Async XLA Ops:
  7.2 162.4 %all-gather.3.cloned.1.call-start = ((), (), s32[]{:S(2)}) async-start(), calls=%async_computation.2 | async-start | bytes 37748736 | tf_op jit(solution)/shard_map/all_gather | solution.py:106
  7.9 352.1 %all-gather.5.cloned.1.call-start = ((), (), s32[]{:S(2)}) async-start(), calls=%async_computation.3 | async-start | bytes 37748736 | tf_op jit(solution)/shard_map/all_gather | solution.py:107
  8.6 1188.0 %reduce-scatter.5.cloned.1.call-start = ((), (), s32[]{:S(2)}) async-start(), calls=%async_computation.5 | async-start | bytes 75497472 | tf_op jit(solution)/shard_map/reduce_scatter | solution.py:113
  10.4 186.8 %copy-start.21 = (f32[1,4096]{1,0:T(1,128)}, f32[1,4096]{1,0:T(1,128)S(1)}, u32[]{:S(2)}) copy-start(f32[1,4096]{1,0:T(1,128)S(1)} %get-tuple-element.39) | copy-start | bytes 49156
  10.4 186.8 %copy-start.27 = (f32[1,4096]{1,0:T(1,128)}, f32[1,4096]{1,0:T(1,128)S(1)}, u32[]{:S(2)}) copy-start(f32[1,4096]{1,0:T(1,128)S(1)} %get-tuple-element.38) | copy-start | bytes 49156
  183.6 13.6 %copy-start.15 = (f32[16,256]{1,0:T(8,128)}, f32[16,256]{1,0:T(8,128)S(1)}, u32[]{:S(2)}) copy-start(f32[16,256]{1,0:T(8,128)S(1)} %broadcast_multiply_fusion) | copy-start | bytes 49156
  197.2 88.7 %copy-start.23 = (f32[16,256]{1,0:T(8,128)}, f32[16,256]{1,0:T(8,128)S(1)}, u32[]{:S(2)}) copy-start(f32[16,256]{1,0:T(8,128)S(1)} %add_rsqrt_fusion) | copy-start | bytes 49156
  528.9 23.1 %copy-start.16 = (f32[16,256]{1,0:T(8,128)S(1)}, f32[16,256]{1,0:T(8,128)}, u32[]{:S(2)}) copy-start(f32[16,256]{1,0:T(8,128)} %copy-done.15) | copy-start | bytes 49156
  528.9 23.1 %copy-start.18 = (f32[1,4096]{1,0:T(1,128)S(1)}, f32[1,4096]{1,0:T(1,128)}, u32[]{:S(2)}) copy-start(f32[1,4096]{1,0:T(1,128)} %get-tuple-element.36) | copy-start | bytes 49156
  528.9 23.1 %copy-start.24 = (f32[16,256]{1,0:T(8,128)S(1)}, f32[16,256]{1,0:T(8,128)}, u32[]{:S(2)}) copy-start(f32[16,256]{1,0:T(8,128)} %copy-done.23) | copy-start | bytes 49156
  528.9 23.1 %copy-start.29 = (f32[1,4096]{1,0:T(1,128)S(1)}, f32[1,4096]{1,0:T(1,128)}, u32[]{:S(2)}) copy-start(f32[1,4096]{1,0:T(1,128)} %get-tuple-element.37) | copy-start | bytes 49156
  528.9 760.3 %reduce-scatter.3.cloned.1.call-start = ((), (), s32[]{:S(2)}) async-start(), calls=%async_computation.4 | async-start | bytes 75497472 | tf_op jit(solution)/shard_map/reduce_scatter | solution.py:112
  631.2 11.3 copy-start.7
  631.2 11.3 copy-start.8
  642.5 13.0 copy-start.9
  647.3 16.3 %copy-start.2 = (bf16[16,256,4,128]{1,3,2,0:T(8,128)(2,1)}, bf16[16,256,4,128]{1,3,2,0:T(8,128)(2,1)S(1)}, u32[]{:S(2)}) copy-start(bf16[16,256,4,128]{1,3,2,0:T(8,128)(2,1)S(1)} %fusion.59) | copy-start | bytes 12582916
  655.5 18.6 %copy-start.31 = (bf16[4,1,128,4096]{3,2,1,0:T(8,128)(2,1)S(1)}, bf16[4,1,128,4096]{3,2,1,0:T(8,128)(2,1)}, u32[]{:S(2)}) copy-start(bf16[4,1,128,4096]{3,2,1,0:T(8,128)(2,1)} %param.10) | copy-start | bytes 12582916
  663.6 112.2 %copy-start.11 = (f32[16,4,256]{2,1,0:T(4,128)}, f32[16,4,256]{2,1,0:T(4,128)S(1)}, u32[]{:S(2)}) copy-start(f32[16,4,256]{2,1,0:T(4,128)S(1)} %get-tuple-element.41) | copy-start | bytes 196612
  674.2 101.7 %copy-start.13 = (f32[16,4,256]{2,1,0:T(4,128)}, f32[16,4,256]{2,1,0:T(4,128)S(1)}, u32[]{:S(2)}) copy-start(f32[16,4,256]{2,1,0:T(4,128)S(1)} %fusion.28) | copy-start | bytes 196612
  726.1 10.1 copy-start
  740.4 23.7 %copy-start.3 = (f32[16,256,4,1,64]{1,4,3,2,0:T(8,128)S(1)}, f32[16,256,4,1,64]{1,4,3,2,0:T(8,128)}, u32[]{:S(2)}) copy-start(f32[16,256,4,1,64]{1,4,3,2,0:T(8,128)} %get-tuple-element.26) | copy-start | bytes 12582916
  754.6 9.6 slice-start
  754.6 9.6 slice-start.1
  754.6 14.6 %slice-start.2 = ((s8[8388608]{0:T(1024)(128)(4,1)}), s8[4194304]{0:T(1024)(128)(4,1)S(1)}, s32[]{:S(2)}) async-start(s8[8388608]{0:T(1024)(128)(4,1)} %bitcast.224), calls=%async_computation.9 | async-start | bytes 8388608
  849.0 498.2 %all-reduce.2.cloned.1.call-start = ((), (), s32[]{:S(2)}) async-start(), calls=%async_computation.6 | async-start | bytes 131072 | tf_op jit(solution)/shard_map/psum | solution.py:119
  922.1 18.1 %copy-start.10 = (pred[256,256]{0,1:T(8,128)(4,1)S(1)}, pred[256,256]{0,1:T(8,128)(4,1)}, u32[]{:S(2)}) copy-start(pred[256,256]{0,1:T(8,128)(4,1)} %iota_compare_fusion) | copy-start | bytes 196612
  922.1 18.1 %copy-start.12 = (f32[16,4,256]{2,1,0:T(4,128)S(1)}, f32[16,4,256]{2,1,0:T(4,128)}, u32[]{:S(2)}) copy-start(f32[16,4,256]{2,1,0:T(4,128)} %copy-done.11) | copy-start | bytes 196612
  922.1 18.1 %copy-start.14 = (f32[16,4,256]{2,1,0:T(4,128)S(1)}, f32[16,4,256]{2,1,0:T(4,128)}, u32[]{:S(2)}) copy-start(f32[16,4,256]{2,1,0:T(4,128)} %copy-done.13) | copy-start | bytes 196612
  981.8 37.1 %copy-start.22 = (f32[1,4096]{1,0:T(1,128)S(1)}, f32[1,4096]{1,0:T(1,128)}, u32[]{:S(2)}) copy-start(f32[1,4096]{1,0:T(1,128)} %copy-done.21) | copy-start | bytes 49156
  981.8 37.1 %copy-start.28 = (f32[1,4096]{1,0:T(1,128)S(1)}, f32[1,4096]{1,0:T(1,128)}, u32[]{:S(2)}) copy-start(f32[1,4096]{1,0:T(1,128)} %copy-done.27) | copy-start | bytes 49156
  1109.8 179.4 %copy-start.20 = (f32[1,4096]{1,0:T(1,128)S(1)}, f32[1,4096]{1,0:T(1,128)}, u32[]{:S(2)}) copy-start(f32[1,4096]{1,0:T(1,128)} %get-tuple-element.36) | copy-start | bytes 49156
  1196.6 104.7 %copy-start.26 = (f32[16,32]{1,0:T(8,128)S(1)}, f32[16,32]{1,0:T(8,128)}, u32[]{:S(2)}) copy-start(f32[16,32]{1,0:T(8,128)} %constant_dynamic-slice_fusion) | copy-start | bytes 6148
  (12 other events, 49.9 us)
Sparse Core Ops, SparseCore 0:
  9.8 159.7 all-gather.2
  171.4 156.9 all-gather.4
  529.0 378.4 reduce-scatter.4
  910.8 378.3 reduce-scatter.2
  1301.4 45.7 all-reduce.1
where the time goes:
time: 1360 us
  matrix products  760 us (56%)
  waiting for transfers between devices  285 us (21%)
  other arithmetic  246 us (18%)
  local copies, waits for them, and re-layouts  49.6 us (4%)
  between operations  14.3 us (1%)
    all_gather x1, waiting for transfers between devices, device_step(): full_in = lax.all_gather(layer_in, 'tp', axis=1, tiled=True)  159 us
    reduce_scatter x1, waiting for transfers between devices, device_step(): lax.psum_scatter(attn_part, 'tp', scatter_dimension=1, tiled=True)  92.6 us
    dot_general x1, matrix products, branch_grads(): jnp.einsum('bsd,bsf->df', mlp_in, hidden_grad, preferred_element_type=jnp...  90.9 us
    dot_general x1, matrix products, branch_grads(): jnp.einsum('bsd,fd->bsf', full_grad, w_down, preferred_element_type=jnp.f...  89.7 us
    dot_general x1, matrix products, branch_grads(): jnp.einsum('bsd,df->bsf', mlp_in, w_up, preferred_element_type=jnp.float32)  88.6 us
    dot_general x1, matrix products, branch_grads(): jnp.einsum('bsf,bsd->fd', act_vals.astype(jnp.bfloat16), full_grad, prefe...  86.8 us
    dot_general x1, matrix products, branch_grads(): jnp.einsum('bsf,df->bsd', hidden_grad, w_up, preferred_element_type=jnp.f...  79.1 us
    another operation x1, other arithmetic, exact_gelu(): return jax.nn.gelu(pre_vals, approximate=False)  74.2 us
  transfers between devices with their start and end apart: 5, of which 3 were waited for; matrix products, arithmetic and copies ran while one was open for 64% of the time, Pallas kernels for 0%

commit v1 on v0

v1 whole, which is shorter than its diff:
```python
import functools
import math

import jax
import jax.numpy as jnp
from jax import lax
from jax.experimental import pallas as pl
from jax.experimental.pallas import tpu as pltpu
from jax.sharding import PartitionSpec as P


NORM_EPS = 1e-5
ROPE_BASE = 10000.0
NEG_BIG = -1e30
SIZES = (4, 6, 6)
VMEM = 62 * 1024 * 1024
F32 = jnp.float32
BF16 = jnp.bfloat16


def dot(lhs, rhs, lc, rc):
    return lax.dot_general(lhs, rhs, (((lc,), (rc,)), ((), ())), preferred_element_type=F32)


def rope_tables(seq_len, head_dim):
    half_dim = head_dim // 2
    inv_freq = ROPE_BASE ** (-2.0 * jnp.arange(half_dim, dtype=F32) / head_dim)
    angles = jnp.arange(seq_len, dtype=F32)[:, None] * inv_freq[None, :]
    sin = jnp.sin(angles)
    cos = jnp.cos(angles)
    return jnp.concatenate([cos, cos], axis=-1), jnp.concatenate([-sin, sin], axis=-1)


def attention_kernel(heads, head_dim, qkv_ref, dc_ref, cos_ref, sin_ref, c_ref, dqkv_ref):
    seq = qkv_ref.shape[1]
    half = head_dim // 2
    width = heads * head_dim
    scale = head_dim ** -0.5
    cos = cos_ref[...]
    sin = sin_ref[...]
    causal = lax.broadcasted_iota(jnp.int32, (seq, seq), 0) >= lax.broadcasted_iota(jnp.int32, (seq, seq), 1)
    for h in range(heads):
        cols = slice(h * head_dim, (h + 1) * head_dim)
        k_cols = slice(width + h * head_dim, width + (h + 1) * head_dim)
        v_cols = slice(2 * width + h * head_dim, 2 * width + (h + 1) * head_dim)
        q = qkv_ref[0, :, cols].astype(F32)
        k = qkv_ref[0, :, k_cols].astype(F32)
        v = qkv_ref[0, :, v_cols]
        dc = dc_ref[0, :, cols]
        q2 = (q * cos + pltpu.roll(q, half, 1) * sin).astype(BF16)
        k2 = (k * cos + pltpu.roll(k, half, 1) * sin).astype(BF16)
        scores = dot(q2, k2, 1, 1) * scale
        scores = jnp.where(causal, scores, NEG_BIG)
        weights = jnp.exp(scores - jnp.max(scores, axis=-1, keepdims=True))
        probs = weights / jnp.sum(weights, axis=-1, keepdims=True)
        probs_bf16 = probs.astype(BF16)
        c_ref[0, :, cols] = dot(probs_bf16, v, 1, 0).astype(BF16)
        dpr = dot(dc, v, 1, 1)
        ds = probs * (dpr - jnp.sum(dpr * probs, axis=-1, keepdims=True))
        ds = (ds * scale).astype(BF16)
        dq2 = dot(ds, k2, 1, 0)
        dk2 = dot(ds, q2, 0, 0)
        dv = dot(probs_bf16, dc, 0, 0)
        dqkv_ref[0, :, cols] = (dq2 * cos - pltpu.roll(dq2, half, 1) * sin).astype(BF16)
        dqkv_ref[0, :, k_cols] = (dk2 * cos - pltpu.roll(dk2, half, 1) * sin).astype(BF16)
        dqkv_ref[0, :, v_cols] = dv.astype(BF16)


def attention_grads(qkv, dc, cos, sin, head_dim):
    batch, seq, qkv_width = qkv.shape
    width = qkv_width // 3
    heads = width // head_dim
    flops = batch * heads * 6 * 2 * seq * seq * head_dim
    return pl.pallas_call(
        functools.partial(attention_kernel, heads, head_dim),
        grid=(batch,),
        in_specs=[
            pl.BlockSpec((1, seq, qkv_width), lambda b: (b, 0, 0)),
            pl.BlockSpec((1, seq, width), lambda b: (b, 0, 0)),
            pl.BlockSpec((seq, head_dim), lambda b: (0, 0)),
            pl.BlockSpec((seq, head_dim), lambda b: (0, 0)),
        ],
        out_specs=[
            pl.BlockSpec((1, seq, width), lambda b: (b, 0, 0)),
            pl.BlockSpec((1, seq, qkv_width), lambda b: (b, 0, 0)),
        ],
        out_shape=[jax.ShapeDtypeStruct((batch, seq, width), BF16), jax.ShapeDtypeStruct(qkv.shape, BF16)],
        cost_estimate=pl.CostEstimate(flops=flops * 3, bytes_accessed=batch * seq * width * 16, transcendentals=batch * heads * seq * seq),
        name="attention_grads",
    )(qkv, dc, cos, sin)


def params_for(**kw):
    return pltpu.CompilerParams(vmem_limit_bytes=VMEM, **kw)


def norm_kernel(x_ref, par_ref, a_ref, m_ref, mean_ref, rstd_ref):
    x = x_ref[...].astype(F32)
    mean = jnp.mean(x, axis=-1, keepdims=True)
    centred = x - mean
    rstd = lax.rsqrt(jnp.mean(centred * centred, axis=-1, keepdims=True) + NORM_EPS)
    xh = centred * rstd
    a_ref[...] = (xh * par_ref[0:1, :] + par_ref[1:2, :]).astype(BF16)
    m_ref[...] = (xh * par_ref[2:3, :] + par_ref[3:4, :]).astype(BF16)
    mean_ref[...] = mean
    rstd_ref[...] = rstd


def norm_inputs(x, params):
    rows, dim = x.shape
    bm = 256
    row_spec = pl.BlockSpec((bm, dim), lambda i: (i, 0))
    col_spec = pl.BlockSpec((bm, 1), lambda i: (i, 0))
    return pl.pallas_call(
        norm_kernel,
        grid=(rows // bm,),
        in_specs=[row_spec, pl.BlockSpec((4, dim), lambda i: (0, 0))],
        out_specs=[row_spec, row_spec, col_spec, col_spec],
        out_shape=[jax.ShapeDtypeStruct(x.shape, BF16)] * 2 + [jax.ShapeDtypeStruct((rows, 1), F32)] * 2,
        cost_estimate=pl.CostEstimate(flops=rows * dim * 400, bytes_accessed=rows * dim * 6, transcendentals=0),
        compiler_params=params_for(),
        name="norm_inputs",
    )(x, params)


def matmul_kernel(rhs_dim, l_ref, r_ref, o_ref):
    o_ref[...] = dot(l_ref[...], r_ref[...], 1, rhs_dim).astype(BF16)


def matmul(lhs, rhs, rhs_dim, bm, bn):
    rows, depth = lhs.shape
    n = rhs.shape[1 - rhs_dim]
    rhs_spec = pl.BlockSpec((bn, depth), lambda j, i: (j, 0)) if rhs_dim else pl.BlockSpec((depth, bn), lambda j, i: (0, j))
    return pl.pallas_call(
        functools.partial(matmul_kernel, rhs_dim),
        grid=(n // bn, rows // bm),
        in_specs=[pl.BlockSpec((bm, depth), lambda j, i: (i, 0)), rhs_spec],
        out_specs=pl.BlockSpec((bm, bn), lambda j, i: (i, j)),
        out_shape=jax.ShapeDtypeStruct((rows, n), BF16),
        cost_estimate=pl.CostEstimate(flops=2 * rows * depth * n, bytes_accessed=2 * (rows * depth + depth * n + rows * n), transcendentals=0),
        compiler_params=params_for(),
        name="project",
    )(lhs, rhs)


def mlp_kernel(m_ref, dy_ref, up_ref, down_ref, u_ref, dh_ref):
    pre = dot(m_ref[...], up_ref[...], 1, 0)
    act_grad = dot(dy_ref[...], down_ref[...], 1, 1)
    cdf = 0.5 * (1.0 + lax.erf(pre * math.sqrt(0.5)))
    pdf = jnp.exp(-0.5 * pre * pre) * (1.0 / math.sqrt(2.0 * math.pi))
    u_ref[...] = (pre * cdf).astype(BF16)
    dh_ref[...] = (act_grad * (cdf + pre * pdf)).astype(BF16)


def mlp_hidden(m, dy, w_up, w_down):
    rows, dim = m.shape
    ff = w_up.shape[1]
    bm, bn = 256, 1024
    return pl.pallas_call(
        mlp_kernel,
        grid=(ff // bn, rows // bm),
        in_specs=[
            pl.BlockSpec((bm, dim), lambda j, i: (i, 0)),
            pl.BlockSpec((bm, dim), lambda j, i: (i, 0)),
            pl.BlockSpec((dim, bn), lambda j, i: (0, j)),
            pl.BlockSpec((bn, dim), lambda j, i: (j, 0)),
        ],
        out_specs=[pl.BlockSpec((bm, bn), lambda j, i: (i, j))] * 2,
        out_shape=[jax.ShapeDtypeStruct((rows, ff), BF16)] * 2,
        cost_estimate=pl.CostEstimate(flops=4 * rows * dim * ff, bytes_accessed=4 * (rows * dim + dim * ff + rows * ff), transcendentals=rows * ff),
        compiler_params=params_for(),
        name="mlp_hidden",
    )(m, dy, w_up, w_down)


def cot_kernel(dqkv_ref, dh_ref, wq_ref, wu_ref, x_ref, mean_ref, rstd_ref, par_ref, t_ref, ln_ref):
    da = dot(dqkv_ref[...], wq_ref[...], 1, 1)
    dm = dot(dh_ref[...], wu_ref[...], 1, 1)
    xh = (x_ref[...].astype(F32) - mean_ref[...]) * rstd_ref[...]
    t_ref[...] = da * par_ref[0:1, :] + dm * par_ref[2:3, :]
    first = pl.program_id(1) == 0
    for i, value in enumerate([da * xh, da, dm * xh, dm]):
        total = jnp.sum(value, axis=0, keepdims=True)
        ln_ref[i:i + 1, :] = jnp.where(first, total, total + ln_ref[i:i + 1, :])


def cotangents(dqkv, dh, wq, wu, x, mean, rstd, params):
    rows, qkv_width = dqkv.shape
    ff = dh.shape[1]
    dim = x.shape[1]
    bm, bd = 512, 1024
    return pl.pallas_call(
        cot_kernel,
        grid=(dim // bd, rows // bm),
        in_specs=[
            pl.BlockSpec((bm, qkv_width), lambda j, i: (i, 0)),
            pl.BlockSpec((bm, ff), lambda j, i: (i, 0)),
            pl.BlockSpec((bd, qkv_width), lambda j, i: (j, 0)),
            pl.BlockSpec((bd, ff), lambda j, i: (j, 0)),
            pl.BlockSpec((bm, bd), lambda j, i: (i, j)),
            pl.BlockSpec((bm, 1), lambda j, i: (i, 0)),
            pl.BlockSpec((bm, 1), lambda j, i: (i, 0)),
            pl.BlockSpec((4, bd), lambda j, i: (0, j)),
        ],
        out_specs=[pl.BlockSpec((bm, bd), lambda j, i: (i, j)), pl.BlockSpec((4, bd), lambda j, i: (0, j))],
        out_shape=[jax.ShapeDtypeStruct((rows, dim), F32), jax.ShapeDtypeStruct((4, dim), F32)],
        cost_estimate=pl.CostEstimate(flops=2 * rows * dim * (qkv_width + ff), bytes_accessed=rows * dim * 6 + 2 * (qkv_width + ff) * (dim + rows), transcendentals=0),
        compiler_params=params_for(),
        name="cotangents",
    )(dqkv, dh, wq, wu, x, mean, rstd, params)


def wgrad_kernel(count, *refs):
    lhs, rhs, out_ref = refs[:count], refs[count:2 * count], refs[2 * count]
    total = dot(lhs[0][...], rhs[0][...], 0, 0)
    for i in range(1, count):
        total += dot(lhs[i][...], rhs[i][...], 0, 0)
    out_ref[...] = total.astype(BF16)


def weight_grad(lhs, rhs, bm, bn):
    count = len(lhs)
    rows = sum(v.shape[0] for v in lhs)
    m, n = lhs[0].shape[1], rhs[0].shape[1]
    in_specs = [pl.BlockSpec((v.shape[0], bm), lambda j, i: (0, i)) for v in lhs]
    in_specs += [pl.BlockSpec((v.shape[0], bn), lambda j, i: (0, j)) for v in rhs]
    return pl.pallas_call(
        functools.partial(wgrad_kernel, count),
        grid=(n // bn, m // bm),
        in_specs=in_specs,
        out_specs=pl.BlockSpec((bm, bn), lambda j, i: (i, j)),
        out_shape=jax.ShapeDtypeStruct((m, n), BF16),
        cost_estimate=pl.CostEstimate(flops=2 * rows * m * n, bytes_accessed=2 * (rows * (m + n) + m * n), transcendentals=0),
        compiler_params=params_for(),
        name="weight_grad",
    )(*lhs, *rhs)


def norm_stats(x):
    mean = jnp.mean(x, axis=-1, keepdims=True)
    centred = x - mean
    return mean, lax.rsqrt(jnp.mean(centred * centred, axis=-1, keepdims=True) + NORM_EPS)


def solution(mesh):
    act_spec = P('dp', 'tp', None)

    def device_step(layer_in, grad_out, w_qkv, w_out, w_up, w_down, ln_params):
        dim = layer_in.shape[2]
        groups, head_dim = w_qkv.shape[1], w_qkv.shape[3]
        width = groups * head_dim
        wq = jnp.swapaxes(w_qkv, 1, 2).reshape(dim, 3 * width)
        wo = w_out.reshape(width, dim)
        bounds = [sum(SIZES[:i]) for i in range(len(SIZES) + 1)]
        slices = [slice(bounds[i], bounds[i + 1]) for i in range(len(SIZES))]
        gathered = []
        for sl in slices:
            x = lax.all_gather(layer_in[sl], 'tp', axis=1, tiled=True)
            dy = lax.all_gather(grad_out[sl], 'tp', axis=1, tiled=True)
            gathered.append((x, dy))
        seq = gathered[0][0].shape[1]
        cos, sin = rope_tables(seq, head_dim)
        saved = []
        ln_parts = []
        owned = []
        for i, nb in enumerate(SIZES):
            rows = nb * seq
            x, dy = (v.reshape(rows, dim) for v in gathered[i])
            if i:
                x, _ = lax.optimization_barrier((x, ln_parts[-1]))
            a, m, mean, rstd = norm_inputs(x, ln_params)
            qkv = matmul(a, wq, 0, 256, 3 * width)
            dc = matmul(dy, wo, 1, 512, width)
            ctx, dqkv = attention_grads(qkv.reshape(nb, seq, 3 * width), dc.reshape(nb, seq, width), cos, sin, head_dim)
            ctx, dqkv = ctx.reshape(rows, width), dqkv.reshape(rows, 3 * width)
            act, dh = mlp_hidden(m, dy, w_up, w_down)
            cot, ln_part = cotangents(dqkv, dh, wq, w_up, x, mean, rstd, ln_params)
            ln_parts.append(ln_part)
            if i == len(SIZES) - 1:
                grad_ln = lax.psum(sum(ln_parts), 'tp')
            owned.append(lax.psum_scatter(cot.reshape(nb, seq, dim), 'tp', scatter_dimension=1, tiled=True))
            saved.append((a, m, dy, act, dh, ctx, dqkv))
        attn_ins, mlp_ins, grads, acts, hiddens, contexts, qkv_grads = zip(*saved)
        outs = []
        for sl, own in zip(slices, owned):
            x = layer_in[sl].astype(F32)
            mean, rstd = norm_stats(x)
            xh = (x - mean) * rstd
            inner = own - jnp.mean(own, axis=-1, keepdims=True) - xh * jnp.mean(own * xh, axis=-1, keepdims=True)
            outs.append((grad_out[sl].astype(F32) + rstd * inner).astype(BF16))
        grad_in = jnp.concatenate(outs, axis=0)
        grad_qkv = weight_grad(attn_ins, qkv_grads, 512, 1536)
        grad_qkv = jnp.swapaxes(grad_qkv.reshape(dim, 3, groups, head_dim), 1, 2)
        grad_wout = weight_grad(contexts, grads, 512, 1024).reshape(w_out.shape)
        grad_up = weight_grad(mlp_ins, hiddens, 512, 1024)
        grad_down = weight_grad(acts, grads, 512, 1024)
        return grad_in, grad_qkv, grad_wout, grad_up, grad_down, grad_ln

    return jax.shard_map(
        device_step,
        mesh=mesh,
        in_specs=(act_spec, act_spec, P(None, 'tp', None, None), P('tp', None, None, None), P(None, 'tp'), P('tp', None), P(None, None)),
        out_specs=(act_spec, P('dp', 'tp', None, None), P(('dp', 'tp'), None, None, None), P('dp', 'tp'), P(('dp', 'tp'), None), P('dp', None)),
        check_vma=False,
    )
```

time: 1360 us -> 1000 us (0.74)
  Pallas kernels: 0 us -> 825 us
  matrix products: 760 us -> 0 us
  waiting for transfers between devices: 285 us -> 59.9 us
  other arithmetic: 246 us -> 32.9 us
    pallas_call x0 -> x22, Pallas kernels: none -> 825 us  [the longest x4 251 us: weight_grad(): pl.pallas_call(functools.partial(wgrad_kernel, count), grid=(n // bn, m /...]
    dot_general x16 -> x0, matrix products: 760 us -> none  [the longest x1 90.9 us: branch_grads(): jnp.einsum('bsd,bsf->df', mlp_in, hidden_grad, preferred_element_type=jnp...]
    all_gather x2 -> x6, waiting for transfers between devices: 159 us -> 58.7 us  [the longest x3 38.5 us: device_step(): dy = lax.all_gather(grad_out[sl], 'tp', axis=1, tiled=True)]
    another operation x5 -> x0, other arithmetic: 98.2 us -> none  [the longest x1 74.2 us: exact_gelu(): return jax.nn.gelu(pre_vals, approximate=False)]
    reduce_scatter x2 -> x3, waiting for transfers between devices: 92.6 us -> 0.02 us  [device_step(): lax.psum_scatter(cot.reshape(nb, seq, dim), 'tp', scatter_dimension=1, ti...]
    unnamed x81 -> x27, local copies, waits for them, and re-layouts: 47.3 us -> 3.03 us
    reshape x0 -> x2, local copies, waits for them, and re-layouts: none -> 43 us  [the longest x1 22 us: device_step(): grad_qkv = jnp.swapaxes(grad_qkv.reshape(dim, 3, groups, head_dim), 1, 2)]
    mul x2 -> x0, other arithmetic: 37.1 us -> none  [the longest x1 37.1 us: norm_stats(): return (centred * inv_std, inv_std)]
  transfers between devices with their start and end apart: 5 -> 10, of which waited for: 3 -> 2; matrix products, arithmetic and copies ran while one was open for 64% -> 9% of each run, Pallas kernels for 0% -> 83%
where the time goes in v1:
time: 1000 us; the launch traced here: 992 us
  Pallas kernels  825 us (82%)
  waiting for transfers between devices  59.9 us (6%)
  local copies, waits for them, and re-layouts  58.6 us (6%)
  other arithmetic  32.9 us (3%)
  between operations  14.8 us (1%)
    pallas_call x4, Pallas kernels, weight_grad(): pl.pallas_call(functools.partial(wgrad_kernel, count), grid=(n // bn, m /...  251 us
    pallas_call x3, Pallas kernels, mlp_hidden(): pl.pallas_call(mlp_kernel, grid=(ff // bn, rows // bm), in_specs=[pl.Bloc...  182 us
    pallas_call x3, Pallas kernels, cotangents(): pl.pallas_call(cot_kernel, grid=(dim // bd, rows // bm), in_specs=[pl.Blo...  176 us
    pallas_call x6, Pallas kernels, matmul(): pl.pallas_call(functools.partial(matmul_kernel, rhs_dim), grid=(n // bn,...  108 us
    pallas_call x3, Pallas kernels, norm_inputs(): pl.pallas_call(norm_kernel, grid=(rows // bm,), in_specs=[row_spec, pl.Bl...  55.6 us
    pallas_call x3, Pallas kernels, attention_grads(): pl.pallas_call(functools.partial(attention_kernel, heads, head_dim), grid...  52.4 us
    all_gather x3, waiting for transfers between devices, device_step(): dy = lax.all_gather(grad_out[sl], 'tp', axis=1, tiled=True)  38.5 us
    reshape x1, local copies, waits for them, and re-layouts, device_step(): grad_qkv = jnp.swapaxes(grad_qkv.reshape(dim, 3, groups, head_dim), 1, 2)  22 us
  transfers between devices with their start and end apart: 10, of which 2 were waited for; matrix products, arithmetic and copies ran while one was open for 9% of the time, Pallas kernels for 83%

profile of v1, /device:TPU:0, one launch (start us, length us, event | category | flops | bytes accessed | tf_op | source)
XLA Modules:
  0.0 991.8 jit_solution(5937960881446614054)
XLA Ops:
  11.9 3.9 fusion.36
  15.9 4.0 fusion.35
  21.1 21.1 %reshape.153.r_ref.wq_ref = bf16[4096,1536]{1,0:T(8,128)(2,1)} reshape(bf16[4096,3,4,128]{3,2,1,0:T(4,128)(2,1)} %bitcast.30) | data formatting | bytes 25165824 | tf_op jit(solution)/shard_map/reshape | solution.py:252
  43.6 20.2 %all-gather.7.cloned.1.call-done = bf16[4,256,4096]{2,1,0:T(8,128)(2,1)} async-done(((bf16[4,32,4096]{2,1,0:T(8,128)(2,1)}), bf16[4,256,4096]{2,1,0:T(8,128)(2,1)}) %all-gather.7.cloned.1.call-update) | async-done | bytes 8388624 | tf_op jit(solution)/shard_map/all_gather | solution.py:258
  63.8 14.5 %norm_inputs.3 = (bf16[1024,4096]{1,0:T(8,128)(2,1)}, bf16[1024,4096]{1,0:T(8,128)(2,1)}, f32[1024,1]{1,0:T(8,128)}, f32[1024,1]{1,0:T(8,128)}) custom-call(bf16[1024,4096]{1,0:T(8,128)(2,1)} %bitcast.36, f32[4,4096]{1,0:T(4,128)} %par_ref.11), custom_call_target="tpu_custom_call" | custom-call | flops 1677721600 | bytes 25165824 | tf_op jit(solution)/shard_map/norm_inputs/pallas_call | solution.py:114
  78.2 38.5 %all-gather.9.cloned.1.call-done = bf16[4,256,4096]{2,1,0:T(8,128)(2,1)} async-done(((bf16[4,32,4096]{2,1,0:T(8,128)(2,1)}), bf16[4,256,4096]{2,1,0:T(8,128)(2,1)}) %all-gather.9.cloned.1.call-update) | async-done | bytes 8388624 | tf_op jit(solution)/shard_map/all_gather | solution.py:259
  116.7 9.0 project.7
  125.7 20.3 %project.6 = bf16[1024,1536]{1,0:T(8,128)(2,1)} custom-call(bf16[1024,4096]{1,0:T(8,128)(2,1)} %get-tuple-element.38.l_ref.refs_0_, bf16[4096,1536]{1,0:T(8,128)(2,1)} %reshape.153.r_ref.wq_ref), custom_call_target="tpu_custom_call" | custom-call | flops 12884901888 | bytes 24117248 | tf_op jit(solution)/shard_map/project/pallas_call | solution.py:134
  146.1 13.6 %attention_grads.3 = (bf16[4,256,512]{2,1,0:T(8,128)(2,1)}, bf16[4,256,1536]{2,1,0:T(8,128)(2,1)}) custom-call(bf16[4,256,1536]{2,1,0:T(8,128)(2,1)} %bitcast.62, bf16[4,256,512]{2,1,0:T(8,128)(2,1)} %bitcast.68, f32[256,128]{1,0:T(8,128)} %get-tuple-element.92.cos_ref, f32[256,128]{1,0:T(8,128)} %get-tuple-element.93.sin_ref), custom_call_target="tpu_custom_call" | custom-call | flops 4831838208 | bytes 8388608 | tf_op jit(solution)/shard_map/attention_grads/pallas_call | solution.py:74
  159.6 48.0 %mlp_hidden.3 = (bf16[1024,2048]{1,0:T(8,128)(2,1)}, bf16[1024,2048]{1,0:T(8,128)(2,1)}) custom-call(bf16[1024,4096]{1,0:T(8,128)(2,1)} %get-tuple-element.40.m_ref.refs_0_, bf16[1024,4096]{1,0:T(8,128)(2,1)} %bitcast.47, bf16[4096,2048]{1,0:T(8,128)(2,1)} %wu_ref.5, bf16[2048,4096]{1,0:T(8,128)(2,1)} %down_ref.5), custom_call_target="tpu_custom_call" | custom-call | flops 34359738368 | bytes 58720256 | tf_op jit(solution)/shard_map/mlp_hidden/pallas_call | solution.py:159
  207.7 46.6 %cotangents.3 = (f32[1024,4096]{1,0:T(8,128)}, f32[4,4096]{1,0:T(4,128)}) custom-call(bf16[1024,1536]{1,0:T(8,128)(2,1)} %bitcast.60, bf16[1024,2048]{1,0:T(8,128)(2,1)} %get-tuple-element.41.dh_ref.refs_3_, bf16[4096,1536]{1,0:T(8,128)(2,1)} %reshape.153.r_ref.wq_ref, bf16[4096,2048]{1,0:T(8,128)(2,1)} %wu_ref.5, bf16[1024,4096]{1,0:T(8,128)(2,1)} %bitcast.37, ...), custom_call_target="tpu_custom_call" | custom-call | flops 30064771072 | bytes 61865984 | tf_op jit(solution)/shard_map/cotangents/pallas_call | solution.py:192
  254.4 20.5 %norm_inputs.4 = (bf16[1536,4096]{1,0:T(8,128)(2,1)}, bf16[1536,4096]{1,0:T(8,128)(2,1)}, f32[1536,1]{1,0:T(8,128)}, f32[1536,1]{1,0:T(8,128)}) custom-call(bf16[1536,4096]{1,0:T(8,128)(2,1)} %bitcast.33, f32[4,4096]{1,0:T(4,128)} %par_ref.11), custom_call_target="tpu_custom_call" | custom-call | flops 2516582400 | bytes 37748736 | tf_op jit(solution)/shard_map/norm_inputs/pallas_call | solution.py:114
  274.9 11.4 %project.9 = bf16[1536,512]{1,0:T(8,128)(2,1)} custom-call(bf16[1536,4096]{1,0:T(8,128)(2,1)} %bitcast.38, bf16[512,4096]{1,0:T(8,128)(2,1)} %bitcast.51), custom_call_target="tpu_custom_call" | custom-call | flops 6442450944 | bytes 18350080 | tf_op jit(solution)/shard_map/project/pallas_call | solution.py:134
  286.3 28.6 %project.8 = bf16[1536,1536]{1,0:T(8,128)(2,1)} custom-call(bf16[1536,4096]{1,0:T(8,128)(2,1)} %get-tuple-element.47.l_ref.refs_1_, bf16[4096,1536]{1,0:T(8,128)(2,1)} %reshape.153.r_ref.wq_ref), custom_call_target="tpu_custom_call" | custom-call | flops 19327352832 | bytes 29884416 | tf_op jit(solution)/shard_map/project/pallas_call | solution.py:134
  315.0 19.3 %attention_grads.4 = (bf16[6,256,512]{2,1,0:T(8,128)(2,1)}, bf16[6,256,1536]{2,1,0:T(8,128)(2,1)}) custom-call(bf16[6,256,1536]{2,1,0:T(8,128)(2,1)} %bitcast.58, bf16[6,256,512]{2,1,0:T(8,128)(2,1)} %bitcast.66, f32[256,128]{1,0:T(8,128)} %get-tuple-element.92.cos_ref, f32[256,128]{1,0:T(8,128)} %get-tuple-element.93.sin_ref), custom_call_target="tpu_custom_call" | custom-call | flops 7247757312 | bytes 12582912 | tf_op jit(solution)/shard_map/attention_grads/pallas_call | solution.py:74
  334.3 67.3 %mlp_hidden.4 = (bf16[1536,2048]{1,0:T(8,128)(2,1)}, bf16[1536,2048]{1,0:T(8,128)(2,1)}) custom-call(bf16[1536,4096]{1,0:T(8,128)(2,1)} %get-tuple-element.49.m_ref.refs_1_, bf16[1536,4096]{1,0:T(8,128)(2,1)} %bitcast.39, bf16[4096,2048]{1,0:T(8,128)(2,1)} %wu_ref.5, bf16[2048,4096]{1,0:T(8,128)(2,1)} %down_ref.5), custom_call_target="tpu_custom_call" | custom-call | flops 51539607552 | bytes 71303168 | tf_op jit(solution)/shard_map/mlp_hidden/pallas_call | solution.py:159
  401.5 66.0 %cotangents.4 = (f32[1536,4096]{1,0:T(8,128)}, f32[4,4096]{1,0:T(4,128)}) custom-call(bf16[1536,1536]{1,0:T(8,128)(2,1)} %bitcast.53, bf16[1536,2048]{1,0:T(8,128)(2,1)} %get-tuple-element.50.dh_ref.refs_4_, bf16[4096,1536]{1,0:T(8,128)(2,1)} %reshape.153.r_ref.wq_ref, bf16[4096,2048]{1,0:T(8,128)(2,1)} %wu_ref.5, bf16[1536,4096]{1,0:T(8,128)(2,1)} %bitcast.34, ...), custom_call_target="tpu_custom_call" | custom-call | flops 45097156608 | bytes 78118912 | tf_op jit(solution)/shard_map/cotangents/pallas_call | solution.py:192
  467.7 20.6 %norm_inputs.5 = (bf16[1536,4096]{1,0:T(8,128)(2,1)}, bf16[1536,4096]{1,0:T(8,128)(2,1)}, f32[1536,1]{1,0:T(8,128)}, f32[1536,1]{1,0:T(8,128)}) custom-call(bf16[1536,4096]{1,0:T(8,128)(2,1)} %bitcast.31, f32[4,4096]{1,0:T(4,128)} %par_ref.11), custom_call_target="tpu_custom_call" | custom-call | flops 2516582400 | bytes 37748736 | tf_op jit(solution)/shard_map/norm_inputs/pallas_call | solution.py:114
  488.3 11.6 %project.11 = bf16[1536,512]{1,0:T(8,128)(2,1)} custom-call(bf16[1536,4096]{1,0:T(8,128)(2,1)} %bitcast.42, bf16[512,4096]{1,0:T(8,128)(2,1)} %bitcast.52), custom_call_target="tpu_custom_call" | custom-call | flops 6442450944 | bytes 18350080 | tf_op jit(solution)/shard_map/project/pallas_call | solution.py:134
  499.9 27.0 %project.10 = bf16[1536,1536]{1,0:T(8,128)(2,1)} custom-call(bf16[1536,4096]{1,0:T(8,128)(2,1)} %get-tuple-element.56.l_ref.refs_2_, bf16[4096,1536]{1,0:T(8,128)(2,1)} %reshape.153.r_ref.wq_ref), custom_call_target="tpu_custom_call" | custom-call | flops 19327352832 | bytes 29884416 | tf_op jit(solution)/shard_map/project/pallas_call | solution.py:134
  526.8 19.5 %attention_grads.5 = (bf16[6,256,512]{2,1,0:T(8,128)(2,1)}, bf16[6,256,1536]{2,1,0:T(8,128)(2,1)}) custom-call(bf16[6,256,1536]{2,1,0:T(8,128)(2,1)} %bitcast.57, bf16[6,256,512]{2,1,0:T(8,128)(2,1)} %bitcast.65, f32[256,128]{1,0:T(8,128)} %get-tuple-element.92.cos_ref, f32[256,128]{1,0:T(8,128)} %get-tuple-element.93.sin_ref), custom_call_target="tpu_custom_call" | custom-call | flops 7247757312 | bytes 12582912 | tf_op jit(solution)/shard_map/attention_grads/pallas_call | solution.py:74
  546.4 67.1 %mlp_hidden.5 = (bf16[1536,2048]{1,0:T(8,128)(2,1)}, bf16[1536,2048]{1,0:T(8,128)(2,1)}) custom-call(bf16[1536,4096]{1,0:T(8,128)(2,1)} %get-tuple-element.58.m_ref.refs_2_, bf16[1536,4096]{1,0:T(8,128)(2,1)} %bitcast.43, bf16[4096,2048]{1,0:T(8,128)(2,1)} %wu_ref.5, bf16[2048,4096]{1,0:T(8,128)(2,1)} %down_ref.5), custom_call_target="tpu_custom_call" | custom-call | flops 51539607552 | bytes 71303168 | tf_op jit(solution)/shard_map/mlp_hidden/pallas_call | solution.py:159
  613.5 63.3 %cotangents.5 = (f32[1536,4096]{1,0:T(8,128)}, f32[4,4096]{1,0:T(4,128)}) custom-call(bf16[1536,1536]{1,0:T(8,128)(2,1)} %bitcast.55, bf16[1536,2048]{1,0:T(8,128)(2,1)} %get-tuple-element.59.dh_ref.refs_5_, bf16[4096,1536]{1,0:T(8,128)(2,1)} %reshape.153.r_ref.wq_ref, bf16[4096,2048]{1,0:T(8,128)(2,1)} %wu_ref.5, bf16[1536,4096]{1,0:T(8,128)(2,1)} %bitcast.32, ...), custom_call_target="tpu_custom_call" | custom-call | flops 45097156608 | bytes 78118912 | tf_op jit(solution)/shard_map/cotangents/pallas_call | solution.py:192
  686.8 66.2 %weight_grad.4 = bf16[4096,1536]{1,0:T(8,128)(2,1)} custom-call(bf16[1024,4096]{1,0:T(8,128)(2,1)} %get-tuple-element.38.l_ref.refs_0_, bf16[1536,4096]{1,0:T(8,128)(2,1)} %get-tuple-element.47.l_ref.refs_1_, bf16[1536,4096]{1,0:T(8,128)(2,1)} %get-tuple-element.56.l_ref.refs_2_, bf16[1024,1536]{1,0:T(8,128)(2,1)} %bitcast.61, bf16[1536,1536]{1,0:T(8,128)(2,1)} %bitcast.54, ...), custom_call_target="tpu_custom_call" | custom-call | flops 51539607552 | bytes 58720256 | tf_op jit(solution)/shard_map/weight_grad/pallas_call | solution.py:227
  753.0 22.0 %reshape.172 = bf16[4096,3,4,128]{3,2,1,0:T(4,128)(2,1)} reshape(bf16[4096,1536]{1,0:T(8,128)(2,1)} %weight_grad.4) | data formatting | bytes 25165824 | tf_op jit(solution)/shard_map/reshape | solution.py:293
  775.7 79.4 %weight_grad.6 = bf16[4096,2048]{1,0:T(8,128)(2,1)} custom-call(bf16[1024,4096]{1,0:T(8,128)(2,1)} %get-tuple-element.40.m_ref.refs_0_, bf16[1536,4096]{1,0:T(8,128)(2,1)} %get-tuple-element.49.m_ref.refs_1_, bf16[1536,4096]{1,0:T(8,128)(2,1)} %get-tuple-element.58.m_ref.refs_2_, bf16[1024,2048]{1,0:T(8,128)(2,1)} %get-tuple-element.41.dh_ref.refs_3_, ...), custom_call_target="tpu_custom_call" | custom-call | flops 68719476736 | bytes 67108864 | tf_op jit(solution)/shard_map/weight_grad/pallas_call | solution.py:227
  855.1 24.7 %weight_grad.5 = bf16[512,4096]{1,0:T(8,128)(2,1)} custom-call(bf16[1024,512]{1,0:T(8,128)(2,1)} %bitcast.67, bf16[1536,512]{1,0:T(8,128)(2,1)} %bitcast.63, bf16[1536,512]{1,0:T(8,128)(2,1)} %bitcast.64, bf16[1024,4096]{1,0:T(8,128)(2,1)} %bitcast.48, bf16[1536,4096]{1,0:T(8,128)(2,1)} %bitcast.40, bf16[1536,4096]{1,0:T(8,128)(2,1)} %bitcast.44), custom_call_target="tpu_custom_call" | custom-call | flops 17179869184 | bytes 41943040 | tf_op jit(solution)/shard_map/weight_grad/pallas_call | solution.py:227
  879.8 80.5 %weight_grad.7 = bf16[2048,4096]{1,0:T(8,128)(2,1)} custom-call(bf16[1024,2048]{1,0:T(8,128)(2,1)} %get-tuple-element.66.refs_0_, bf16[1536,2048]{1,0:T(8,128)(2,1)} %get-tuple-element.67.refs_1_, bf16[1536,2048]{1,0:T(8,128)(2,1)} %get-tuple-element.68.refs_2_, bf16[1024,4096]{1,0:T(8,128)(2,1)} %bitcast.49, bf16[1536,4096]{1,0:T(8,128)(2,1)} %bitcast.41, ...), custom_call_target="tpu_custom_call" | custom-call | flops 68719476736 | bytes 67108864 | tf_op jit(solution)/shard_map/weight_grad/pallas_call | solution.py:227
  962.9 3.4 fusion.28
  966.4 3.9 fusion.8
  972.3 3.2 fusion.33
  975.9 4.7 fusion.12
  (80 shorter events, 26.8 us)
Async XLA Ops:
  7.2 56.6 %all-gather.7.cloned.1.call-start = ((), (), s32[]{:S(2)}) async-start(), calls=%async_computation.3 | async-start | bytes 9437184 | tf_op jit(solution)/shard_map/all_gather | solution.py:258
  9.5 107.2 %all-gather.9.cloned.1.call-start = ((), (), s32[]{:S(2)}) async-start(), calls=%async_computation.4 | async-start | bytes 9437184 | tf_op jit(solution)/shard_map/all_gather | solution.py:259
  11.9 242.5 %all-gather.11.cloned.1.call-start = ((), (), s32[]{:S(2)}) async-start(), calls=%async_computation.6 | async-start | bytes 14155776 | tf_op jit(solution)/shard_map/all_gather | solution.py:258
  15.9 259.0 %all-gather.13.cloned.1.call-start = ((), (), s32[]{:S(2)}) async-start(), calls=%async_computation.7 | async-start | bytes 14155776 | tf_op jit(solution)/shard_map/all_gather | solution.py:259
  19.9 447.7 %all-gather.15.cloned.1.call-start = ((), (), s32[]{:S(2)}) async-start(), calls=%async_computation.9 | async-start | bytes 14155776 | tf_op jit(solution)/shard_map/all_gather | solution.py:258
  20.5 467.7 %all-gather.17.cloned.1.call-start = ((), (), s32[]{:S(2)}) async-start(), calls=%async_computation.10 | async-start | bytes 14155776 | tf_op jit(solution)/shard_map/all_gather | solution.py:259
  21.1 939.3 %reduce-scatter.4.cloned.1.call-start = ((), (), s32[]{:S(2)}) async-start(), calls=%async_computation.5 | async-start | bytes 18874368 | tf_op jit(solution)/shard_map/reduce_scatter | solution.py:281
  254.3 712.0 %reduce-scatter.6.cloned.1.call-start = ((), (), s32[]{:S(2)}) async-start(), calls=%async_computation.8 | async-start | bytes 28311552 | tf_op jit(solution)/shard_map/reduce_scatter | solution.py:281
  467.6 504.7 %reduce-scatter.8.cloned.1.call-start = ((), (), s32[]{:S(2)}) async-start(), calls=%async_computation.11 | async-start | bytes 28311552 | tf_op jit(solution)/shard_map/reduce_scatter | solution.py:281
  676.8 306.1 %all-reduce.2.cloned.1.call-start = ((), (), s32[]{:S(2)}) async-start(), calls=%async_computation.12 | async-start | bytes 131072 | tf_op jit(solution)/shard_map/psum | solution.py:280
  678.3 0.6 copy-start.10
  683.2 0.6 copy-start.7
  753.0 22.0 %copy-start.4 = (f32[4,4096]{1,0:T(4,128)S(1)}, f32[4,4096]{1,0:T(4,128)}, u32[]{:S(2)}) copy-start(f32[4,4096]{1,0:T(4,128)} %get-tuple-element.45) | copy-start | bytes 196612
  753.0 22.0 %copy-start.5 = (f32[4,4096]{1,0:T(4,128)S(1)}, f32[4,4096]{1,0:T(4,128)}, u32[]{:S(2)}) copy-start(f32[4,4096]{1,0:T(4,128)} %get-tuple-element.54) | copy-start | bytes 196612
  753.0 22.0 %copy-start.6 = (f32[4,4096]{1,0:T(4,128)S(1)}, f32[4,4096]{1,0:T(4,128)}, u32[]{:S(2)}) copy-start(f32[4,4096]{1,0:T(4,128)} %get-tuple-element.69) | copy-start | bytes 196612
  879.8 80.5 %copy-start.11 = (f32[4,32]{1,0:T(4,128)S(1)}, f32[4,32]{1,0:T(4,128)}, u32[]{:S(2)}) copy-start(f32[4,32]{1,0:T(4,128)} %copy-done.10) | copy-start | bytes 1540
  879.8 80.5 %copy-start.12 = (f32[4,32]{1,0:T(4,128)S(1)}, f32[4,32]{1,0:T(4,128)}, u32[]{:S(2)}) copy-start(f32[4,32]{1,0:T(4,128)} %add_rsqrt_fusion.2) | copy-start | bytes 1540
  960.4 2.6 copy-start.2
  962.9 3.5 copy-start.8
  962.9 3.5 copy-start.9
  966.4 9.2 copy-start.1
  972.3 3.6 copy-start
  975.9 4.8 copy-start.3
Sparse Core Ops, SparseCore 0:
  10.4 53.2 all-gather.6
  66.2 50.5 all-gather.8
  119.2 68.2 all-gather.10
  189.2 68.2 all-gather.12
  259.2 68.2 all-gather.14
  329.2 68.2 all-gather.16
  401.0 110.5 reduce-scatter.3
  515.2 150.4 reduce-scatter.5
  676.9 150.8 reduce-scatter.7
  855.2 46.2 all-reduce.1

commit v2 on v1

v2 whole, which is shorter than its diff:
```python
import functools
import math

import jax
import jax.numpy as jnp
from jax import lax
from jax.experimental import pallas as pl
from jax.experimental.pallas import tpu as pltpu
from jax.sharding import PartitionSpec as P


NORM_EPS = 1e-5
ROPE_BASE = 10000.0
NEG_BIG = -1e30
SIZES = (4, 6, 6)
VMEM = 63 * 1024 * 1024
F32 = jnp.float32
BF16 = jnp.bfloat16


def dot(lhs, rhs, lc, rc):
    return lax.dot_general(lhs, rhs, (((lc,), (rc,)), ((), ())), preferred_element_type=F32)


def rope_tables(seq_len, head_dim):
    half_dim = head_dim // 2
    inv_freq = ROPE_BASE ** (-2.0 * jnp.arange(half_dim, dtype=F32) / head_dim)
    angles = jnp.arange(seq_len, dtype=F32)[:, None] * inv_freq[None, :]
    sin = jnp.sin(angles)
    cos = jnp.cos(angles)
    return jnp.concatenate([cos, cos], axis=-1), jnp.concatenate([-sin, sin], axis=-1)


def attention_kernel(heads, head_dim, qkv_ref, dc_ref, cos_ref, sin_ref, c_ref, dqkv_ref):
    seq = qkv_ref.shape[1]
    half = head_dim // 2
    width = heads * head_dim
    scale = head_dim ** -0.5
    cos = cos_ref[...]
    sin = sin_ref[...]
    causal = lax.broadcasted_iota(jnp.int32, (seq, seq), 0) >= lax.broadcasted_iota(jnp.int32, (seq, seq), 1)
    each = range(heads)

    def cols(h, kind):
        return slice(kind * width + h * head_dim, kind * width + (h + 1) * head_dim)

    def rope(t):
        return (t * cos + pltpu.roll(t, half, 1) * sin).astype(BF16)

    def rope_back(t):
        return (t * cos - pltpu.roll(t, half, 1) * sin).astype(BF16)

    q2 = [rope(qkv_ref[0, :, cols(h, 0)].astype(F32)) for h in each]
    k2 = [rope(qkv_ref[0, :, cols(h, 1)].astype(F32)) for h in each]
    v = [qkv_ref[0, :, cols(h, 2)] for h in each]
    dc = [dc_ref[0, :, cols(h, 0)] for h in each]
    scores = [dot(q2[h], k2[h], 1, 1) for h in each]
    dpr = [dot(dc[h], v[h], 1, 1) for h in each]
    scores = [jnp.where(causal, t * scale, NEG_BIG) for t in scores]
    weights = [jnp.exp(t - jnp.max(t, axis=-1, keepdims=True)) for t in scores]
    probs = [t * (1.0 / jnp.sum(t, axis=-1, keepdims=True)) for t in weights]
    probs_bf16 = [t.astype(BF16) for t in probs]
    for h in each:
        c_ref[0, :, cols(h, 0)] = dot(probs_bf16[h], v[h], 1, 0).astype(BF16)
    for h in each:
        dqkv_ref[0, :, cols(h, 2)] = dot(probs_bf16[h], dc[h], 0, 0).astype(BF16)
    ds = [(probs[h] * (dpr[h] - jnp.sum(dpr[h] * probs[h], axis=-1, keepdims=True)) * scale).astype(BF16) for h in each]
    for h in each:
        dqkv_ref[0, :, cols(h, 0)] = rope_back(dot(ds[h], k2[h], 1, 0))
    for h in each:
        dqkv_ref[0, :, cols(h, 1)] = rope_back(dot(ds[h], q2[h], 0, 0))


def attention_grads(qkv, dc, cos, sin, head_dim):
    batch, seq, qkv_width = qkv.shape
    width = qkv_width // 3
    heads = width // head_dim
    flops = batch * heads * 6 * 2 * seq * seq * head_dim
    return pl.pallas_call(
        functools.partial(attention_kernel, heads, head_dim),
        grid=(batch,),
        in_specs=[
            pl.BlockSpec((1, seq, qkv_width), lambda b: (b, 0, 0)),
            pl.BlockSpec((1, seq, width), lambda b: (b, 0, 0)),
            pl.BlockSpec((seq, head_dim), lambda b: (0, 0)),
            pl.BlockSpec((seq, head_dim), lambda b: (0, 0)),
        ],
        out_specs=[
            pl.BlockSpec((1, seq, width), lambda b: (b, 0, 0)),
            pl.BlockSpec((1, seq, qkv_width), lambda b: (b, 0, 0)),
        ],
        out_shape=[jax.ShapeDtypeStruct((batch, seq, width), BF16), jax.ShapeDtypeStruct(qkv.shape, BF16)],
        cost_estimate=pl.CostEstimate(flops=flops * 3, bytes_accessed=batch * seq * width * 16, transcendentals=batch * heads * seq * seq),
        compiler_params=params_for(),
        name="attention_grads",
    )(qkv, dc, cos, sin)


def params_for(**kw):
    return pltpu.CompilerParams(vmem_limit_bytes=VMEM, **kw)


def staged(groups, body):
    first = pl.program_id(0) == 0

    @pl.when(first)
    def _():
        for group in groups:
            for copy in group:
                copy.start()
        for n, group in enumerate(groups):
            for copy in group:
                copy.wait()
            body(n)

    @pl.when(jnp.logical_not(first))
    def _():
        for n in range(len(groups)):
            body(n)


def hbm():
    return pl.BlockSpec(memory_space=pl.ANY)


def row_blocks(bm, width):
    return pl.BlockSpec((bm, width), lambda i: (i, 0))


def norm_qkv_kernel(bn, parts, x_ref, w_hbm, par_ref, a_ref, m_ref, mean_ref, rstd_ref, qkv_ref, w_vmem, sem):
    copies = [
        pltpu.make_async_copy(w_hbm.at[:, pl.ds(n * bn, bn)], w_vmem.at[:, pl.ds(n * bn, bn)], sem.at[n])
        for n in range(qkv_ref.shape[1] // bn)
    ]
    first = pl.program_id(0) == 0
    size = x_ref.shape[0] // parts

    def norm(part):
        rows = slice(part * size, (part + 1) * size)
        x = x_ref[rows, :].astype(F32)
        mean = jnp.mean(x, axis=-1, keepdims=True)
        centred = x - mean
        rstd = lax.rsqrt(jnp.mean(centred * centred, axis=-1, keepdims=True) + NORM_EPS)
        xh = centred * rstd
        a_ref[rows, :] = (xh * par_ref[0:1, :] + par_ref[1:2, :]).astype(BF16)
        m_ref[rows, :] = (xh * par_ref[2:3, :] + par_ref[3:4, :]).astype(BF16)
        mean_ref[rows, :] = mean
        rstd_ref[rows, :] = rstd

    @pl.when(first)
    def _():
        for copy in copies:
            copy.start()

    norm(0)

    @pl.when(first)
    def _():
        for copy in copies:
            copy.wait()

    for part in range(parts):
        rows = slice(part * size, (part + 1) * size)
        qkv_ref[rows, :] = dot(a_ref[rows, :], w_vmem[...], 1, 0).astype(BF16)
        if part + 1 < parts:
            norm(part + 1)


def norm_qkv(x, wq, params):
    rows, dim = x.shape
    n = wq.shape[1]
    bm, bn = 256, 512
    return pl.pallas_call(
        functools.partial(norm_qkv_kernel, bn, 2),
        grid=(rows // bm,),
        in_specs=[row_blocks(bm, dim), hbm(), pl.BlockSpec((4, dim), lambda i: (0, 0))],
        out_specs=[row_blocks(bm, dim), row_blocks(bm, dim), row_blocks(bm, 1), row_blocks(bm, 1), row_blocks(bm, n)],
        out_shape=[jax.ShapeDtypeStruct(x.shape, BF16)] * 2 + [jax.ShapeDtypeStruct((rows, 1), F32)] * 2 + [jax.ShapeDtypeStruct((rows, n), BF16)],
        scratch_shapes=[pltpu.VMEM(wq.shape, BF16), pltpu.SemaphoreType.DMA((n // bn,))],
        cost_estimate=pl.CostEstimate(flops=2 * rows * dim * (n + 200), bytes_accessed=rows * dim * 6 + 2 * n * (rows + dim), transcendentals=0),
        compiler_params=params_for(),
        name="norm_qkv",
    )(x, wq, params)


def mlp_kernel(bn, m_ref, dy_ref, up_hbm, down_hbm, out_hbm, u_ref, dh_ref, dc_ref, up_vmem, down_vmem, out_vmem, sem):
    count = u_ref.shape[1] // bn
    piece = [pl.ds(n * bn, bn) for n in range(count)]
    groups = [
        [
            pltpu.make_async_copy(up_hbm.at[:, piece[n]], up_vmem.at[:, piece[n]], sem.at[0, n]),
            pltpu.make_async_copy(down_hbm.at[piece[n], :], down_vmem.at[piece[n], :], sem.at[1, n]),
        ]
        for n in range(count)
    ]
    groups.append([pltpu.make_async_copy(out_hbm, out_vmem, sem.at[0, count])])

    def body(n):
        if n == count:
            dc_ref[...] = dot(dy_ref[...], out_vmem[...], 1, 1).astype(BF16)
            return
        pre = dot(m_ref[...], up_vmem[:, piece[n]], 1, 0)
        act_grad = dot(dy_ref[...], down_vmem[piece[n], :], 1, 1)
        cdf = 0.5 * (1.0 + lax.erf(pre * math.sqrt(0.5)))
        pdf = jnp.exp(-0.5 * pre * pre) * (1.0 / math.sqrt(2.0 * math.pi))
        cols = slice(n * bn, (n + 1) * bn)
        u_ref[:, cols] = (pre * cdf).astype(BF16)
        dh_ref[:, cols] = (act_grad * (cdf + pre * pdf)).astype(BF16)

    staged(groups, body)


def mlp_hidden(m, dy, w_up, w_down, wo):
    rows, dim = m.shape
    ff, width = w_up.shape[1], wo.shape[0]
    bm, bn = 256, 512
    return pl.pallas_call(
        functools.partial(mlp_kernel, bn),
        grid=(rows // bm,),
        in_specs=[row_blocks(bm, dim), row_blocks(bm, dim), hbm(), hbm(), hbm()],
        out_specs=[row_blocks(bm, ff), row_blocks(bm, ff), row_blocks(bm, width)],
        out_shape=[jax.ShapeDtypeStruct((rows, ff), BF16)] * 2 + [jax.ShapeDtypeStruct((rows, width), BF16)],
        scratch_shapes=[
            pltpu.VMEM(w_up.shape, BF16),
            pltpu.VMEM(w_down.shape, BF16),
            pltpu.VMEM(wo.shape, BF16),
            pltpu.SemaphoreType.DMA((2, ff // bn + 1)),
        ],
        cost_estimate=pl.CostEstimate(flops=2 * rows * dim * (2 * ff + width), bytes_accessed=4 * (rows * dim + dim * ff + rows * ff), transcendentals=rows * ff),
        compiler_params=params_for(),
        name="mlp_hidden",
    )(m, dy, w_up, w_down, wo)


def cot_kernel(bd, dqkv_ref, dh_ref, wq_hbm, wu_hbm, x_ref, mean_ref, rstd_ref, par_ref, t_ref, ln_ref, wq_vmem, wu_vmem, sem):
    count = t_ref.shape[1] // bd
    piece = [pl.ds(n * bd, bd) for n in range(count)]
    groups = [
        [
            pltpu.make_async_copy(wq_hbm.at[piece[n], :], wq_vmem.at[piece[n], :], sem.at[0, n]),
            pltpu.make_async_copy(wu_hbm.at[piece[n], :], wu_vmem.at[piece[n], :], sem.at[1, n]),
        ]
        for n in range(count)
    ]

    @pl.when(pl.program_id(0) == 0)
    def _():
        ln_ref[...] = jnp.zeros_like(ln_ref)

    def body(n):
        cols = slice(n * bd, (n + 1) * bd)
        da = dot(dqkv_ref[...], wq_vmem[piece[n], :], 1, 1)
        dm = dot(dh_ref[...], wu_vmem[piece[n], :], 1, 1)
        xh = (x_ref[:, cols].astype(F32) - mean_ref[...]) * rstd_ref[...]
        t_ref[:, cols] = da * par_ref[0:1, cols] + dm * par_ref[2:3, cols]
        for i, value in enumerate([da * xh, da, dm * xh, dm]):
            ln_ref[i:i + 1, cols] += jnp.sum(value, axis=0, keepdims=True)

    staged(groups, body)


def cotangents(dqkv, dh, wq, wu, x, mean, rstd, params):
    rows, qkv_width = dqkv.shape
    ff = dh.shape[1]
    dim = x.shape[1]
    bm, bd = 256, 512
    whole = pl.BlockSpec((4, dim), lambda i: (0, 0))
    return pl.pallas_call(
        functools.partial(cot_kernel, bd),
        grid=(rows // bm,),
        in_specs=[row_blocks(bm, qkv_width), row_blocks(bm, ff), hbm(), hbm(), row_blocks(bm, dim), row_blocks(bm, 1), row_blocks(bm, 1), whole],
        out_specs=[row_blocks(bm, dim), whole],
        out_shape=[jax.ShapeDtypeStruct((rows, dim), F32), jax.ShapeDtypeStruct((4, dim), F32)],
        scratch_shapes=[pltpu.VMEM(wq.shape, BF16), pltpu.VMEM(wu.shape, BF16), pltpu.SemaphoreType.DMA((2, dim // bd))],
        cost_estimate=pl.CostEstimate(flops=2 * rows * dim * (qkv_width + ff), bytes_accessed=rows * dim * 6 + 2 * (qkv_width + ff) * (dim + rows), transcendentals=0),
        compiler_params=params_for(),
        name="cotangents",
    )(dqkv, dh, wq, wu, x, mean, rstd, params)


def chunk_copies(rhs, rhs_vmem, sem, bn):
    offsets = [sum(v.shape[0] for v in rhs[:i]) for i in range(len(rhs))]
    spans = [pl.ds(o, v.shape[0]) for o, v in zip(offsets, rhs)]
    groups = [
        [pltpu.make_async_copy(v.at[:, pl.ds(n * bn, bn)], rhs_vmem.at[span, pl.ds(n * bn, bn)], sem.at[c, n]) for c, (v, span) in enumerate(zip(rhs, spans))]
        for n in range(rhs_vmem.shape[1] // bn)
    ]
    return groups, spans


def wgrad_kernel(count, bn, *refs):
    lhs, rhs = refs[:count], refs[count:2 * count]
    out_ref, rhs_vmem, sem = refs[2 * count:]
    groups, spans = chunk_copies(rhs, rhs_vmem, sem, bn)

    def body(n):
        cols = pl.ds(n * bn, bn)
        total = dot(lhs[0][...], rhs_vmem[spans[0], cols], 0, 0)
        for c in range(1, count):
            total += dot(lhs[c][...], rhs_vmem[spans[c], cols], 0, 0)
        out_ref[:, n * bn:(n + 1) * bn] = total.astype(BF16)

    staged(groups, body)


def weight_grad(lhs, rhs):
    count = len(lhs)
    rows = sum(v.shape[0] for v in lhs)
    m, n = lhs[0].shape[1], rhs[0].shape[1]
    bm, bn = 256, 512
    return pl.pallas_call(
        functools.partial(wgrad_kernel, count, bn),
        grid=(m // bm,),
        in_specs=[pl.BlockSpec((v.shape[0], bm), lambda i: (0, i)) for v in lhs] + [hbm()] * count,
        out_specs=row_blocks(bm, n),
        out_shape=jax.ShapeDtypeStruct((m, n), BF16),
        scratch_shapes=[pltpu.VMEM((rows, n), BF16), pltpu.SemaphoreType.DMA((count, n // bn))],
        cost_estimate=pl.CostEstimate(flops=2 * rows * m * n, bytes_accessed=2 * (rows * (m + n) + m * n), transcendentals=0),
        compiler_params=params_for(),
        name="weight_grad",
    )(*lhs, *rhs)


def wgrad_pair_kernel(count, split, bn, *refs):
    lhs_a, lhs_b, rhs = refs[:count], refs[count:2 * count], refs[2 * count:3 * count]
    out_a, out_b, rhs_vmem, sem = refs[3 * count:]
    groups, spans = chunk_copies(rhs, rhs_vmem, sem, bn)

    def run(lhs, out, n):
        cols = pl.ds(n * bn, bn)
        total = dot(lhs[0][...], rhs_vmem[spans[0], cols], 0, 0)
        for c in range(1, count):
            total += dot(lhs[c][...], rhs_vmem[spans[c], cols], 0, 0)
        out[:, n * bn:(n + 1) * bn] = total.astype(BF16)

    @pl.when(pl.program_id(0) < split)
    def _():
        staged(groups, lambda n: run(lhs_a, out_a, n))

    @pl.when(pl.program_id(0) >= split)
    def _():
        for n in range(len(groups)):
            run(lhs_b, out_b, n)


def weight_grad_pair(lhs_a, lhs_b, rhs):
    count = len(rhs)
    rows = sum(v.shape[0] for v in rhs)
    ma, mb, n = lhs_a[0].shape[1], lhs_b[0].shape[1], rhs[0].shape[1]
    bm, bn = 256, 512
    split, total = ma // bm, (ma + mb) // bm
    at_a = lambda i: jnp.minimum(i, split - 1)
    at_b = lambda i: jnp.maximum(i - split, 0)
    return pl.pallas_call(
        functools.partial(wgrad_pair_kernel, count, split, bn),
        grid=(total,),
        in_specs=[pl.BlockSpec((v.shape[0], bm), lambda i: (0, at_a(i))) for v in lhs_a]
        + [pl.BlockSpec((v.shape[0], bm), lambda i: (0, at_b(i))) for v in lhs_b]
        + [hbm()] * count,
        out_specs=[pl.BlockSpec((bm, n), lambda i: (at_a(i), 0)), pl.BlockSpec((bm, n), lambda i: (at_b(i), 0))],
        out_shape=[jax.ShapeDtypeStruct((ma, n), BF16), jax.ShapeDtypeStruct((mb, n), BF16)],
        scratch_shapes=[pltpu.VMEM((rows, n), BF16), pltpu.SemaphoreType.DMA((count, n // bn))],
        cost_estimate=pl.CostEstimate(flops=2 * rows * (ma + mb) * n, bytes_accessed=2 * (rows * (ma + mb + n) + (ma + mb) * n), transcendentals=0),
        compiler_params=params_for(),
        name="weight_grad_pair",
    )(*lhs_a, *lhs_b, *rhs)


def wgrad_qkv_kernel(count, *refs):
    lhs, rhs = refs[:count], refs[count:2 * count]
    out_ref, rhs_vmem, rows_vmem, sem = refs[2 * count:]
    bm, kinds, heads, head_dim = out_ref.shape
    bn = heads * head_dim
    groups, spans = chunk_copies(rhs, rhs_vmem, sem, bn)

    def body(n):
        cols = pl.ds(n * bn, bn)
        total = dot(lhs[0][...], rhs_vmem[spans[0], cols], 0, 0)
        for c in range(1, count):
            total += dot(lhs[c][...], rhs_vmem[spans[c], cols], 0, 0)
        for h in range(heads):
            rows_vmem[pl.ds(n * heads + h, bm, stride=kinds * heads), :] = total[:, h * head_dim:(h + 1) * head_dim]

    staged(groups, body)
    out_ref[...] = rows_vmem[...].astype(BF16).reshape(out_ref.shape)


def weight_grad_qkv(lhs, rhs, kinds, heads, head_dim):
    count = len(lhs)
    rows = sum(v.shape[0] for v in lhs)
    m, n = lhs[0].shape[1], rhs[0].shape[1]
    bm = 256
    return pl.pallas_call(
        functools.partial(wgrad_qkv_kernel, count),
        grid=(m // bm,),
        in_specs=[pl.BlockSpec((v.shape[0], bm), lambda i: (0, i)) for v in lhs] + [hbm()] * count,
        out_specs=pl.BlockSpec((bm, kinds, heads, head_dim), lambda i: (i, 0, 0, 0)),
        out_shape=jax.ShapeDtypeStruct((m, kinds, heads, head_dim), BF16),
        scratch_shapes=[pltpu.VMEM((rows, n), BF16), pltpu.VMEM((bm * kinds * heads, head_dim), F32), pltpu.SemaphoreType.DMA((count, kinds))],
        cost_estimate=pl.CostEstimate(flops=2 * rows * m * n, bytes_accessed=2 * (rows * (m + n) + m * n), transcendentals=0),
        compiler_params=params_for(),
        name="weight_grad_qkv",
    )(*lhs, *rhs)


def final_kernel(bounds, *refs):
    owned = refs[:-3]
    x_ref, dy_ref, out_ref = refs[-3:]
    step = pl.program_id(0)
    for i, own_ref in enumerate(owned):
        @pl.when(jnp.logical_and(step >= bounds[i], step < bounds[i + 1]))
        def _(own_ref=own_ref):
            x = x_ref[...].astype(F32)
            centred = x - jnp.mean(x, axis=-1, keepdims=True)
            rstd = lax.rsqrt(jnp.mean(centred * centred, axis=-1, keepdims=True) + NORM_EPS)
            xh = centred * rstd
            own = own_ref[...]
            inner = own - jnp.mean(own, axis=-1, keepdims=True) - xh * jnp.mean(own * xh, axis=-1, keepdims=True)
            out_ref[...] = (dy_ref[...].astype(F32) + rstd * inner).astype(BF16)


def input_grad(owned, x, dy, bounds):
    batch, seq, dim = x.shape
    per = math.gcd(*bounds[1:])
    bounds = [b // per for b in bounds]
    block = (per, seq, dim)
    own_specs = [pl.BlockSpec(block, lambda b, lo=bounds[i], hi=bounds[i + 1]: (jnp.clip(b - lo, 0, hi - lo - 1), 0, 0)) for i in range(len(owned))]
    plain = pl.BlockSpec(block, lambda b: (b, 0, 0))
    return pl.pallas_call(
        functools.partial(final_kernel, bounds),
        grid=(batch // per,),
        in_specs=own_specs + [plain, plain],
        out_specs=plain,
        out_shape=jax.ShapeDtypeStruct(x.shape, BF16),
        cost_estimate=pl.CostEstimate(flops=batch * seq * dim * 20, bytes_accessed=batch * seq * dim * 10, transcendentals=0),
        compiler_params=params_for(),
        name="input_grad",
    )(*owned, x, dy)


def butterfly_sum(value, axis, size):
    step = 1
    while step < size:
        value = value + lax.ppermute(value, axis, [(i, i ^ step) for i in range(size)])
        step *= 2
    return value


def solution(mesh):
    act_spec = P('dp', 'tp', None)

    def device_step(layer_in, grad_out, w_qkv, w_out, w_up, w_down, ln_params):
        dim = layer_in.shape[2]
        groups, head_dim = w_qkv.shape[1], w_qkv.shape[3]
        width = groups * head_dim
        wq = jnp.swapaxes(w_qkv, 1, 2).reshape(dim, 3 * width)
        wo = w_out.reshape(width, dim)
        bounds = [sum(SIZES[:i]) for i in range(len(SIZES) + 1)]
        slices = [slice(bounds[i], bounds[i + 1]) for i in range(len(SIZES))]
        gathered = []
        for sl in slices:
            x = lax.all_gather(layer_in[sl], 'tp', axis=1, tiled=True)
            dy = lax.all_gather(grad_out[sl], 'tp', axis=1, tiled=True)
            gathered.append((x, dy))
        seq = gathered[0][0].shape[1]
        cos, sin = rope_tables(seq, head_dim)
        saved = []
        ln_parts = []
        owned = []
        for i, nb in enumerate(SIZES):
            rows = nb * seq
            x, dy = (v.reshape(rows, dim) for v in gathered[i])
            if i:
                x, _ = lax.optimization_barrier((x, ln_parts[-1]))
            a, m, mean, rstd, qkv = norm_qkv(x, wq, ln_params)
            act, dh, dc = mlp_hidden(m, dy, w_up, w_down, wo)
            ctx, dqkv = attention_grads(qkv.reshape(nb, seq, 3 * width), dc.reshape(nb, seq, width), cos, sin, head_dim)
            ctx, dqkv = ctx.reshape(rows, width), dqkv.reshape(rows, 3 * width)
            cot, ln_part = cotangents(dqkv, dh, wq, w_up, x, mean, rstd, ln_params)
            ln_parts.append(ln_part)
            if i == len(SIZES) - 1:
                grad_ln = butterfly_sum(sum(ln_parts), 'tp', mesh.shape['tp'])
            owned.append(lax.psum_scatter(cot.reshape(nb, seq, dim), 'tp', scatter_dimension=1, tiled=True))
            saved.append((a, m, dy, act, dh, ctx, dqkv))
        attn_ins, mlp_ins, grads, acts, hiddens, contexts, qkv_grads = zip(*saved)
        grad_qkv = jnp.swapaxes(weight_grad_qkv(attn_ins, qkv_grads, 3, groups, head_dim), 1, 2)
        grad_up = weight_grad(mlp_ins, hiddens)
        grad_down, grad_wout = weight_grad_pair(acts, contexts, grads)
        grad_wout = grad_wout.reshape(w_out.shape)
        grad_in = input_grad(owned, layer_in, grad_out, bounds)
        return grad_in, grad_qkv, grad_wout, grad_up, grad_down, grad_ln

    return jax.shard_map(
        device_step,
        mesh=mesh,
        in_specs=(act_spec, act_spec, P(None, 'tp', None, None), P('tp', None, None, None), P(None, 'tp'), P('tp', None), P(None, None)),
        out_specs=(act_spec, P('dp', 'tp', None, None), P(('dp', 'tp'), None, None, None), P('dp', 'tp'), P(('dp', 'tp'), None), P('dp', None)),
        check_vma=False,
    )
```

time: 1000 us -> 880 us (0.88)
  Pallas kernels: 825 us -> 773 us
  other arithmetic: 32.9 us -> 2.08 us
  local copies, waits for them, and re-layouts: 58.6 us -> 34.4 us
  waiting for transfers between devices: 59.9 us -> 45.4 us
    pallas_call x19 -> x13, Pallas kernels: 773 us -> 741 us  [the longest x3 191 us: mlp_hidden(): pl.pallas_call(functools.partial(mlp_kernel, bn), grid=(rows // bm,), in_...]
    reshape x1 -> x0, local copies, waits for them, and re-layouts: 22 us -> none  [device_step(): grad_qkv = jnp.swapaxes(grad_qkv.reshape(dim, 3, groups, head_dim), 1, 2)]
    pallas_call x3, Pallas kernels: 52.4 us -> 32.3 us  [attention_grads(): pl.pallas_call(functools.partial(attention_kernel, heads, head_dim), grid...]
    reduce_sum x8 -> x0, other arithmetic: 19.2 us -> none  [the longest x3 6.07 us: norm_stats(): jnp.mean(centred * centred, axis=-1, keepdims=True) + NORM_EPS]
    all_gather x3, waiting for transfers between devices: 38.5 us -> 24 us  [device_step(): dy = lax.all_gather(grad_out[sl], 'tp', axis=1, tiled=True)]
  transfers between devices with their start and end apart: 10 -> 12, of which waited for: 2 -> 2; matrix products, arithmetic and copies ran while one was open for 9% -> 4% of each run, Pallas kernels for 83% -> 87%
where the time goes in v2:
time: 880 us; the launch traced here: 873 us
  Pallas kernels  773 us (88%)
  waiting for transfers between devices  45.4 us (5%)
  local copies, waits for them, and re-layouts  34.4 us (4%)
  between operations  14.2 us (2%)
    pallas_call x3, Pallas kernels, mlp_hidden(): pl.pallas_call(functools.partial(mlp_kernel, bn), grid=(rows // bm,), in_...  191 us
    pallas_call x3, Pallas kernels, cotangents(): pl.pallas_call(functools.partial(cot_kernel, bd), grid=(rows // bm,), in_...  168 us
    pallas_call x3, Pallas kernels, norm_qkv(): pl.pallas_call(functools.partial(norm_qkv_kernel, bn, 2), grid=(rows // b...  114 us
    pallas_call x1, Pallas kernels, weight_grad_pair(): pl.pallas_call(functools.partial(wgrad_pair_kernel, count, split, bn), gr...  112 us
    pallas_call x1, Pallas kernels, weight_grad(): pl.pallas_call(functools.partial(wgrad_kernel, count, bn), grid=(m // bm,...  78.7 us
    pallas_call x1, Pallas kernels, weight_grad_qkv(): pl.pallas_call(functools.partial(wgrad_qkv_kernel, count), grid=(m // bm,...  65.1 us
    pallas_call x3, Pallas kernels, attention_grads(): pl.pallas_call(functools.partial(attention_kernel, heads, head_dim), grid...  32.3 us
    all_gather x3, waiting for transfers between devices, device_step(): dy = lax.all_gather(grad_out[sl], 'tp', axis=1, tiled=True)  24 us
  transfers between devices with their start and end apart: 12, of which 2 were waited for; matrix products, arithmetic and copies ran while one was open for 4% of the time, Pallas kernels for 87%

profile of v2, /device:TPU:0, one launch (start us, length us, event | category | flops | bytes accessed | tf_op | source)
XLA Modules:
  0.0 872.9 jit_solution(14694638760946413531)
XLA Ops:
  7.2 2.3 slice.18
  9.6 2.3 slice.19
  11.9 3.9 fusion.4
  15.9 4.0 fusion.3
  20.0 0.5 all-gather.15.cloned.1.call-update
  20.6 0.5 all-gather.17.cloned.1.call-update
  21.1 21.1 %reshape.90.w_hbm.wq_hbm = bf16[4096,1536]{1,0:T(8,128)(2,1)} reshape(bf16[4096,3,4,128]{3,2,1,0:T(4,128)(2,1)} %bitcast.30) | data formatting | bytes 25165824 | tf_op jit(solution)/shard_map/reshape | solution.py:456
  42.2 0.5 fusion.2
  42.7 0.8 pad_maximum_fusion
  43.6 20.2 %all-gather.7.cloned.1.call-done = bf16[4,256,4096]{2,1,0:T(8,128)(2,1)} async-done(((bf16[4,32,4096]{2,1,0:T(8,128)(2,1)}), bf16[4,256,4096]{2,1,0:T(8,128)(2,1)}) %all-gather.7.cloned.1.call-update) | async-done | bytes 8388624 | tf_op jit(solution)/shard_map/all_gather | solution.py:462
  63.8 29.0 %norm_qkv.3 = (bf16[1024,4096]{1,0:T(8,128)(2,1)}, bf16[1024,4096]{1,0:T(8,128)(2,1)}, f32[1024,1]{1,0:T(8,128)}, f32[1024,1]{1,0:T(8,128)}, bf16[1024,1536]{1,0:T(8,128)(2,1)}) custom-call(bf16[1024,4096]{1,0:T(8,128)(2,1)} %bitcast.41, bf16[4096,1536]{1,0:T(8,128)(2,1)} %reshape.90.w_hbm.wq_hbm, f32[4,4096]{1,0:T(4,128)} %par_ref.11), custom_call_target="tpu_custom_call" | custom-call | flops 14562623488 | bytes 40894464 | tf_op jit(solution)/shard_map/norm_qkv/pallas_call | solution.py:173
  92.8 23.9 %all-gather.9.cloned.1.call-done = bf16[4,256,4096]{2,1,0:T(8,128)(2,1)} async-done(((bf16[4,32,4096]{2,1,0:T(8,128)(2,1)}), bf16[4,256,4096]{2,1,0:T(8,128)(2,1)}) %all-gather.9.cloned.1.call-update) | async-done | bytes 8388624 | tf_op jit(solution)/shard_map/all_gather | solution.py:463
  116.7 50.5 %mlp_hidden.3 = (bf16[1024,2048]{1,0:T(8,128)(2,1)}, bf16[1024,2048]{1,0:T(8,128)(2,1)}, bf16[1024,512]{1,0:T(8,128)(2,1)}) custom-call(bf16[1024,4096]{1,0:T(8,128)(2,1)} %get-tuple-element.47.m_ref.refs_0_, bf16[1024,4096]{1,0:T(8,128)(2,1)} %bitcast.39, bf16[4096,2048]{1,0:T(8,128)(2,1)} %wu_hbm.5, bf16[2048,4096]{1,0:T(8,128)(2,1)} %down_hbm.5, ...), custom_call_target="tpu_custom_call" | custom-call | flops 38654705664 | bytes 58720256 | tf_op jit(solution)/shard_map/mlp_hidden/pallas_call | solution.py:217
  167.2 8.5 attention_grads.3
  175.8 42.5 %cotangents.3 = (f32[1024,4096]{1,0:T(8,128)}, f32[4,4096]{1,0:T(4,128)}) custom-call(bf16[1024,1536]{1,0:T(8,128)(2,1)} %bitcast.54, bf16[1024,2048]{1,0:T(8,128)(2,1)} %get-tuple-element.50.dh_ref.refs_3_, bf16[4096,1536]{1,0:T(8,128)(2,1)} %reshape.90.w_hbm.wq_hbm, bf16[4096,2048]{1,0:T(8,128)(2,1)} %wu_hbm.5, bf16[1024,4096]{1,0:T(8,128)(2,1)} %bitcast.42, ...), custom_call_target="tpu_custom_call" | custom-call | flops 30064771072 | bytes 61865984 | tf_op jit(solution)/shard_map/cotangents/pallas_call | solution.py:268
  218.4 42.3 %norm_qkv.4 = (bf16[1536,4096]{1,0:T(8,128)(2,1)}, bf16[1536,4096]{1,0:T(8,128)(2,1)}, f32[1536,1]{1,0:T(8,128)}, f32[1536,1]{1,0:T(8,128)}, bf16[1536,1536]{1,0:T(8,128)(2,1)}) custom-call(bf16[1536,4096]{1,0:T(8,128)(2,1)} %bitcast.37, bf16[4096,1536]{1,0:T(8,128)(2,1)} %reshape.90.w_hbm.wq_hbm, f32[4,4096]{1,0:T(4,128)} %par_ref.11), custom_call_target="tpu_custom_call" | custom-call | flops 21843935232 | bytes 55050240 | tf_op jit(solution)/shard_map/norm_qkv/pallas_call | solution.py:173
  260.8 70.2 %mlp_hidden.4 = (bf16[1536,2048]{1,0:T(8,128)(2,1)}, bf16[1536,2048]{1,0:T(8,128)(2,1)}, bf16[1536,512]{1,0:T(8,128)(2,1)}) custom-call(bf16[1536,4096]{1,0:T(8,128)(2,1)} %get-tuple-element.57.m_ref.refs_1_, bf16[1536,4096]{1,0:T(8,128)(2,1)} %bitcast.31, bf16[4096,2048]{1,0:T(8,128)(2,1)} %wu_hbm.5, bf16[2048,4096]{1,0:T(8,128)(2,1)} %down_hbm.5, ...), custom_call_target="tpu_custom_call" | custom-call | flops 57982058496 | bytes 71303168 | tf_op jit(solution)/shard_map/mlp_hidden/pallas_call | solution.py:217
  331.0 11.8 %attention_grads.4 = (bf16[6,256,512]{2,1,0:T(8,128)(2,1)}, bf16[6,256,1536]{2,1,0:T(8,128)(2,1)}) custom-call(bf16[6,256,1536]{2,1,0:T(8,128)(2,1)} %bitcast.52, bf16[6,256,512]{2,1,0:T(8,128)(2,1)} %bitcast.60, f32[256,128]{1,0:T(8,128)} %get-tuple-element.99.cos_ref, f32[256,128]{1,0:T(8,128)} %get-tuple-element.100.sin_ref), custom_call_target="tpu_custom_call" | custom-call | flops 7247757312 | bytes 12582912 | tf_op jit(solution)/shard_map/attention_grads/pallas_call | solution.py:79
  342.8 59.0 %cotangents.4 = (f32[1536,4096]{1,0:T(8,128)}, f32[4,4096]{1,0:T(4,128)}) custom-call(bf16[1536,1536]{1,0:T(8,128)(2,1)} %bitcast.47, bf16[1536,2048]{1,0:T(8,128)(2,1)} %get-tuple-element.60.dh_ref.refs_4_, bf16[4096,1536]{1,0:T(8,128)(2,1)} %reshape.90.w_hbm.wq_hbm, bf16[4096,2048]{1,0:T(8,128)(2,1)} %wu_hbm.5, bf16[1536,4096]{1,0:T(8,128)(2,1)} %bitcast.38, ...), custom_call_target="tpu_custom_call" | custom-call | flops 45097156608 | bytes 78118912 | tf_op jit(solution)/shard_map/cotangents/pallas_call | solution.py:268
  401.9 42.6 %norm_qkv.5 = (bf16[1536,4096]{1,0:T(8,128)(2,1)}, bf16[1536,4096]{1,0:T(8,128)(2,1)}, f32[1536,1]{1,0:T(8,128)}, f32[1536,1]{1,0:T(8,128)}, bf16[1536,1536]{1,0:T(8,128)(2,1)}) custom-call(bf16[1536,4096]{1,0:T(8,128)(2,1)} %bitcast.35, bf16[4096,1536]{1,0:T(8,128)(2,1)} %reshape.90.w_hbm.wq_hbm, f32[4,4096]{1,0:T(4,128)} %par_ref.11), custom_call_target="tpu_custom_call" | custom-call | flops 21843935232 | bytes 55050240 | tf_op jit(solution)/shard_map/norm_qkv/pallas_call | solution.py:173
  444.6 70.1 %mlp_hidden.5 = (bf16[1536,2048]{1,0:T(8,128)(2,1)}, bf16[1536,2048]{1,0:T(8,128)(2,1)}, bf16[1536,512]{1,0:T(8,128)(2,1)}) custom-call(bf16[1536,4096]{1,0:T(8,128)(2,1)} %get-tuple-element.67.m_ref.refs_2_, bf16[1536,4096]{1,0:T(8,128)(2,1)} %bitcast.33, bf16[4096,2048]{1,0:T(8,128)(2,1)} %wu_hbm.5, bf16[2048,4096]{1,0:T(8,128)(2,1)} %down_hbm.5, ...), custom_call_target="tpu_custom_call" | custom-call | flops 57982058496 | bytes 71303168 | tf_op jit(solution)/shard_map/mlp_hidden/pallas_call | solution.py:217
  514.7 12.0 %attention_grads.5 = (bf16[6,256,512]{2,1,0:T(8,128)(2,1)}, bf16[6,256,1536]{2,1,0:T(8,128)(2,1)}) custom-call(bf16[6,256,1536]{2,1,0:T(8,128)(2,1)} %bitcast.51, bf16[6,256,512]{2,1,0:T(8,128)(2,1)} %bitcast.59, f32[256,128]{1,0:T(8,128)} %get-tuple-element.99.cos_ref, f32[256,128]{1,0:T(8,128)} %get-tuple-element.100.sin_ref), custom_call_target="tpu_custom_call" | custom-call | flops 7247757312 | bytes 12582912 | tf_op jit(solution)/shard_map/attention_grads/pallas_call | solution.py:79
  526.6 66.0 %cotangents.5 = (f32[1536,4096]{1,0:T(8,128)}, f32[4,4096]{1,0:T(4,128)}) custom-call(bf16[1536,1536]{1,0:T(8,128)(2,1)} %bitcast.49, bf16[1536,2048]{1,0:T(8,128)(2,1)} %get-tuple-element.70.dh_ref.refs_5_, bf16[4096,1536]{1,0:T(8,128)(2,1)} %reshape.90.w_hbm.wq_hbm, bf16[4096,2048]{1,0:T(8,128)(2,1)} %wu_hbm.5, bf16[1536,4096]{1,0:T(8,128)(2,1)} %bitcast.36, ...), custom_call_target="tpu_custom_call" | custom-call | flops 45097156608 | bytes 78118912 | tf_op jit(solution)/shard_map/cotangents/pallas_call | solution.py:268
  592.7 0.8 copy-done
  593.5 0.1 collective-permute-start
  593.6 112.4 %weight_grad_pair.1 = (bf16[2048,4096]{1,0:T(8,128)(2,1)}, bf16[512,4096]{1,0:T(8,128)(2,1)}) custom-call(bf16[1024,2048]{1,0:T(8,128)(2,1)} %get-tuple-element.77.refs_0_, bf16[1536,2048]{1,0:T(8,128)(2,1)} %get-tuple-element.78.refs_1_, bf16[1536,2048]{1,0:T(8,128)(2,1)} %get-tuple-element.79.refs_2_, bf16[1024,512]{1,0:T(8,128)(2,1)} %bitcast.61, ...), custom_call_target="tpu_custom_call" | custom-call | flops 85899345920 | bytes 75497472 | tf_op jit(solution)/shard_map/weight_grad_pair/pallas_call | solution.py:354
  706.1 1.4 collective-permute-start.1
  707.5 78.7 %weight_grad.1 = bf16[4096,2048]{1,0:T(8,128)(2,1)} custom-call(bf16[1024,4096]{1,0:T(8,128)(2,1)} %get-tuple-element.47.m_ref.refs_0_, bf16[1536,4096]{1,0:T(8,128)(2,1)} %get-tuple-element.57.m_ref.refs_1_, bf16[1536,4096]{1,0:T(8,128)(2,1)} %get-tuple-element.67.m_ref.refs_2_, bf16[1024,2048]{1,0:T(8,128)(2,1)} %get-tuple-element.50.dh_ref.refs_3_, ...), custom_call_target="tpu_custom_call" | custom-call | flops 68719476736 | bytes 67108864 | tf_op jit(solution)/shard_map/weight_grad/pallas_call | solution.py:311
  786.2 1.4 collective-permute-start.2
  787.7 65.1 %weight_grad_qkv.1 = bf16[4096,3,4,128]{3,2,1,0:T(4,128)(2,1)} custom-call(bf16[1024,4096]{1,0:T(8,128)(2,1)} %get-tuple-element.74.refs_0_, bf16[1536,4096]{1,0:T(8,128)(2,1)} %get-tuple-element.75.refs_1_, bf16[1536,4096]{1,0:T(8,128)(2,1)} %get-tuple-element.76.refs_2_, bf16[1024,1536]{1,0:T(8,128)(2,1)} %bitcast.55, bf16[1536,1536]{1,0:T(8,128)(2,1)} %bitcast.48, ...), custom_call_target="tpu_custom_call" | custom-call | flops 51539607552 | bytes 58720256 | tf_op jit(solution)/shard_map/weight_grad_qkv/pallas_call | solution.py:393
  852.7 0.6 add.25
  853.4 12.8 %input_grad.1 = bf16[16,32,4096]{2,1,0:T(8,128)(2,1)} custom-call(f32[4,32,4096]{2,1,0:T(8,128)} %reduce-scatter.4.cloned.1.call-done.refs_0_, f32[6,32,4096]{2,1,0:T(8,128)} %reduce-scatter.6.cloned.1.call-done.refs_1_, f32[6,32,4096]{2,1,0:T(8,128)} %reduce-scatter.8.cloned.1.call-done.refs_2_, bf16[16,32,4096]{2,1,0:T(8,128)(2,1)} %refs_3_.1, ...), custom_call_target="tpu_custom_call" | custom-call | flops 41943040 | bytes 20971520 | tf_op jit(solution)/shard_map/input_grad/pallas_call | solution.py:429
  (35 shorter events, 0.7 us)
Async XLA Ops:
  7.2 56.6 %all-gather.7.cloned.1.call-start = ((), (), s32[]{:S(2)}) async-start(), calls=%async_computation.3 | async-start | bytes 9437184 | tf_op jit(solution)/shard_map/all_gather | solution.py:462
  9.5 107.2 %all-gather.9.cloned.1.call-start = ((), (), s32[]{:S(2)}) async-start(), calls=%async_computation.4 | async-start | bytes 9437184 | tf_op jit(solution)/shard_map/all_gather | solution.py:463
  11.9 206.5 %all-gather.11.cloned.1.call-start = ((), (), s32[]{:S(2)}) async-start(), calls=%async_computation.6 | async-start | bytes 14155776 | tf_op jit(solution)/shard_map/all_gather | solution.py:462
  15.9 244.9 %all-gather.13.cloned.1.call-start = ((), (), s32[]{:S(2)}) async-start(), calls=%async_computation.7 | async-start | bytes 14155776 | tf_op jit(solution)/shard_map/all_gather | solution.py:463
  19.9 382.0 %all-gather.15.cloned.1.call-start = ((), (), s32[]{:S(2)}) async-start(), calls=%async_computation.9 | async-start | bytes 14155776 | tf_op jit(solution)/shard_map/all_gather | solution.py:462
  20.5 424.1 %all-gather.17.cloned.1.call-start = ((), (), s32[]{:S(2)}) async-start(), calls=%async_computation.10 | async-start | bytes 14155776 | tf_op jit(solution)/shard_map/all_gather | solution.py:463
  21.1 832.3 %reduce-scatter.4.cloned.1.call-start = ((), (), s32[]{:S(2)}) async-start(), calls=%async_computation.5 | async-start | bytes 18874368 | tf_op jit(solution)/shard_map/reduce_scatter | solution.py:483
  218.3 635.0 %reduce-scatter.6.cloned.1.call-start = ((), (), s32[]{:S(2)}) async-start(), calls=%async_computation.8 | async-start | bytes 28311552 | tf_op jit(solution)/shard_map/reduce_scatter | solution.py:483
  401.9 451.5 %reduce-scatter.8.cloned.1.call-start = ((), (), s32[]{:S(2)}) async-start(), calls=%async_computation.11 | async-start | bytes 28311552 | tf_op jit(solution)/shard_map/reduce_scatter | solution.py:483
  592.6 0.8 copy-start
  592.6 0.9 copy-start.1
  592.6 0.9 copy-start.2
  593.5 112.5 %collective-permute-start = (f32[4,4096]{1,0:T(4,128)S(1)}, f32[4,4096]{1,0:T(4,128)S(1)}, u32[]{:S(2)}, u32[]{:S(2)}) collective-permute-start(f32[4,4096]{1,0:T(4,128)S(1)} %add_add_fusion), channel_id=1, source_target_pairs={{0,1},{1,0},{2,3},{3,2},{4,5},{5,4},{6,7},{7,6},{8,9},{9,8},{10,11... | collective-permute-start | bytes 196616 | tf_op jit(solution)/shard_map/ppermute | solution.py:444
  706.1 80.1 %collective-permute-start.1 = (f32[4,4096]{1,0:T(4,128)S(1)}, f32[4,4096]{1,0:T(4,128)S(1)}, u32[]{:S(2)}, u32[]{:S(2)}) collective-permute-start(f32[4,4096]{1,0:T(4,128)S(1)} %add.23), channel_id=1, source_target_pairs={{0,2},{1,3},{2,0},{3,1},{4,6},{5,7},{6,4},{7,5},{8,10},{9,11},{10,... | collective-permute-start | bytes 196616 | tf_op jit(solution)/shard_map/ppermute | solution.py:444
  786.2 66.5 %collective-permute-start.2 = (f32[4,4096]{1,0:T(4,128)S(1)}, f32[4,4096]{1,0:T(4,128)S(1)}, u32[]{:S(2)}, u32[]{:S(2)}) collective-permute-start(f32[4,4096]{1,0:T(4,128)S(1)} %add.24), channel_id=1, source_target_pairs={{0,4},{1,5},{2,6},{3,7},{4,0},{5,1},{6,2},{7,3},{8,12},{9,13},{10,... | collective-permute-start | bytes 196616 | tf_op jit(solution)/shard_map/ppermute | solution.py:444
Sparse Core Ops, SparseCore 0:
  10.4 53.3 all-gather.6
  66.2 50.5 all-gather.8
  119.2 68.2 all-gather.10
  189.2 68.2 all-gather.12
  259.2 68.2 all-gather.14
  329.2 68.2 all-gather.16
  401.0 110.5 reduce-scatter.3
  515.2 150.4 reduce-scatter.5
  669.2 152.8 reduce-scatter.7
